TPU v7x, 32 devices: a whole 2x2x4 slice. The times are simulated.
32 devices in a mesh: row: 8 (over z, y), ta: 4 (over x, core).
Axes of the slice: x: 2, y: 2, z: 4, core: 2. Of those that a mesh axis runs over, the one named last changes fastest.
Arguments:
- hidden: bfloat16 [8, 256, 3584], P('row', None, 'ta'), may hold values from -6 to 6
- target: bfloat16 [8, 256, 3584], P('row', None, 'ta'), may hold values from -6 to 6
- w_down: bfloat16 [8, 2, 3584, 256], P('row', None, 'ta'), may hold values from -5 to 5
- w_up: bfloat16 [8, 2, 256, 3584], P('row', None, None, 'ta'), may hold values from -5 to 5
- m_down: float32 [8, 2, 3584, 256], P('row', None, 'ta'), may hold values from -9 to 9
- m_up: float32 [8, 2, 256, 3584], P('row', None, None, 'ta'), may hold values from -9 to 9
Outputs:
- avg_down: bfloat16 [2, 3584, 256], P(None, 'ta')
- avg_up: bfloat16 [2, 256, 3584], P(None, None, 'ta')
- mom_down: float32 [2, 3584, 256], P(None, 'ta')
- mom_up: float32 [2, 256, 3584], P(None, None, 'ta')
All inputs are finite; a program needn't handle non-finite values.
Results may differ from a plain program's by a relative error of at most 0.019.
Values may be sent and summed in bfloat16 or wider, within the bound.
A program may use at most 128 MiB of HBM per device.

v0:
```python
import functools

import jax
import jax.numpy as jnp
from jax import lax
from jax.experimental import pallas as pl
from jax.experimental.pallas import tpu as pltpu
from jax.sharding import PartitionSpec as P

MESH = pl.DeviceIdType.MESH
STEPS = 4
norm_eps = 1e-06
learn_rate = 0.02
moment_decay = 0.9


def dot_nn(a, b):
    return jnp.dot(a, b, preferred_element_type=jnp.float32)


def dot_nt(a, b):
    return lax.dot_general(a, b, (((1,), (1,)), ((), ())), preferred_element_type=jnp.float32)


def row_bits(replicas, *lengths):
    if replicas & (replicas - 1) or any(length % (16 * replicas) for length in lengths):
        return []
    return [2**k for k in range(replicas.bit_length() - 1)]


def fused_kernel(
    shards, replicas,
    x0_ref, tg_ref, wd_in, wu_in, md_in, mu_in,
    wd_out, wu_out, md_out, mu_out,
    wd, wu, md, mu, wdl, wul, mdl, mul, res_wd, res_wu, res_md, res_mu,
    got_wd, got_wu, got_md, got_mu, row_send, row_recv,
    x1, xt, gr, pre, act, inv, tot, sqs, low,
    s1, r1, s2, r2, s3, r3, q1, p1, q2, p2, q3, p3,
    main_send, main_recv, side_send, side_recv,
):
    tok, width = x0_ref.shape
    rank = wd.shape[2]
    full = width * shards
    half = tok // 2
    chips = shards // 2
    me = lax.axis_index("ta")
    core = lax.rem(me, 2)
    sibling = me + 1 - 2 * core
    partners = [lax.rem(me + 2 * k, shards) for k in range(1, chips)]
    d_scale = full ** (-0.5)
    r_scale = rank ** (-0.5)

    barrier = pltpu.get_barrier_semaphore()
    for peer in [sibling] + partners:
        pl.semaphore_signal(barrier, inc=1, device_id={"ta": peer}, device_id_type=MESH)
    bits = row_bits(replicas, width, rank)
    levels = len(bits)
    spot = lax.axis_index("row")
    own_bit = {bit: lax.rem(spot // bit, 2) for bit in bits}
    row_peer = {bit: spot + bit - 2 * bit * own_bit[bit] for bit in bits}
    for bit in bits:
        pl.semaphore_signal(barrier, inc=1, device_id={"row": row_peer[bit]}, device_id_type=MESH)
    pl.semaphore_wait(barrier, chips + levels)

    wd[...] = wd_in[...]
    wu[...] = wu_in[...]
    md[...] = md_in[...]
    mu[...] = mu_in[...]

    mine = pl.ds(pl.multiple_of(core * half, half), half)
    other = pl.ds(pl.multiple_of((1 - core) * half, half), half)

    def send(src, dst, sems, index, peer):
        copy = pltpu.make_async_remote_copy(
            src_ref=src, dst_ref=dst,
            send_sem=sems[0].at[index], recv_sem=sems[1].at[index],
            device_id={"ta": peer}, device_id_type=MESH,
        )
        copy.start()
        return copy

    main = (main_send, main_recv)
    side = (side_send, side_recv)

    def to_row(column):
        return jnp.broadcast_to(column, (half, half)).T[0:8]

    def to_column(row):
        return jnp.broadcast_to(row[0:1, :], (half, half)).T[:, 0:1]

    def exchange(parity, value, squares, work):
        tot[...] = value
        s1[...] = tot[other, :].astype(jnp.bfloat16)
        copies = [send(s1, r1, main, 0, sibling)]
        if squares is not None:
            sqs[...] = squares
            q1[...] = to_row(sqs[other, :])
            copies.append(send(q1, p1, side, 0, sibling))
            own_row = to_row(sqs[mine, :])
        for copy in copies:
            copy.wait()
        pair = tot[mine, :] + r1[...].astype(jnp.float32)
        s2[...] = pair.astype(jnp.bfloat16)
        base = parity * (chips - 1)
        copies = [
            send(s2, r2.at[base + k], main, 1 + base + k, peer) for k, peer in enumerate(partners)
        ]
        if squares is not None:
            pair_row = own_row + p1[...]
            q2[...] = pair_row
            copies += [
                send(q2, p2.at[base + k], side, 1 + base + k, peer)
                for k, peer in enumerate(partners)
            ]
        if work is not None:
            work()
        for copy in copies:
            copy.wait()
        total = pair
        for k in range(chips - 1):
            total = total + r2[base + k].astype(jnp.float32)
        last = 1 + 2 * (chips - 1)
        s3[...] = total.astype(jnp.bfloat16)
        copies = [send(s3, r3, main, last, sibling)]
        tot[mine, :] = total
        if squares is not None:
            row = pair_row
            for k in range(chips - 1):
                row = row + p2[base + k]
            q3[...] = row
            copies.append(send(q3, p3, side, last, sibling))
            sqs[mine, :] = to_column(row)
        for copy in copies:
            copy.wait()
        tot[other, :] = r3[...].astype(jnp.float32)
        if squares is not None:
            sqs[other, :] = to_column(p3[...])

    def forward(layer, rows, wide_rows, work=None):
        squares = jnp.sum(wide_rows * wide_rows, axis=1, keepdims=True)
        exchange(layer, dot_nn(rows, wd[layer]) * d_scale, squares, work)
        inverse = lax.rsqrt(sqs[...] / full + norm_eps)
        preact = tot[...] * inverse
        activation = (preact * jax.nn.sigmoid(preact)).astype(jnp.bfloat16)
        inv[layer] = inverse
        pre[layer] = preact
        act[layer] = activation
        lifted = dot_nn(activation, wu[layer]) * r_scale
        return (wide_rows + lifted).astype(jnp.bfloat16)

    def update(w, m, layer, grad, last):
        moment = moment_decay * m[layer] + grad
        m[layer] = moment
        if last and levels:
            return
        w[layer] = (w[layer].astype(jnp.float32) - learn_rate * moment).astype(jnp.bfloat16)

    def update_up(layer, last):
        update(wu, mu, layer, dot_nn(act[layer].T, gr[...].astype(jnp.bfloat16)) * r_scale, last)

    def low_grads(layer):
        preact = pre[layer]
        sig = jax.nn.sigmoid(preact)
        grad_pre = tot[...] * (sig * (1.0 + preact * (1.0 - sig)))
        low[...] = (grad_pre * inv[layer]).astype(jnp.bfloat16)
        return jnp.sum(grad_pre * preact, axis=1, keepdims=True)

    down, up = (wdl, got_wd, res_wd), (wul, got_wu, res_wu)
    mdown, mup = (mdl, got_md, res_md), (mul, got_mu, res_mu)
    layers = list(reversed(range(wd.shape[0])))
    chunks = [pair + (layer, bits) for layer in layers for pair in (up, down)]
    first = len(chunks)
    swapped = bits[:2][::-1] + bits[2:]
    chunks += [
        pair + (layer, swapped if layer == 0 and pair is mup else bits)
        for layer in layers
        for pair in (mup, mdown)
    ]

    def start(picked):
        for chunk in picked if levels else []:
            row_copy(chunk, 0).start()

    def advance(slot):
        for chunk in range(len(chunks)):
            stage = slot - chunk
            if not levels or stage < 0 or stage >= 2 * levels:
                continue
            row_copy(chunk, stage).wait_recv()
            if stage < levels:
                acc, got, res, layer, order = chunks[chunk]
                size = acc.shape[1] >> (stage + 1)
                keep = pl.ds(region(chunk, stage + 1), size)
                landed = got.at[layer, pl.ds(acc.shape[1] - 2 * size, size)]
                total = acc[layer, keep, :].astype(jnp.float32) + landed[...].astype(jnp.float32)
                if stage < levels - 1:
                    acc[layer, keep, :] = total.astype(jnp.bfloat16)
                else:
                    res[layer, keep, :] = (total * (1.0 / replicas)).astype(jnp.bfloat16)
            if stage < 2 * levels - 1:
                row_copy(chunk, stage + 1).start()

    def region(chunk, depth):
        acc, _, _, _, order = chunks[chunk]
        start = 0
        for k in range(depth):
            start = start + own_bit[order[k]] * (acc.shape[1] >> (k + 1))
        return pl.multiple_of(start, acc.shape[1] >> depth) if depth else 0

    def row_copy(chunk, stage):
        acc, got, res, layer, order = chunks[chunk]
        rows = acc.shape[1]
        if stage < levels:
            bit = order[stage]
            size = rows >> (stage + 1)
            away = region(chunk, stage) + (1 - own_bit[bit]) * size
            src = acc.at[layer, pl.ds(pl.multiple_of(away, size), size)]
            dst = got.at[layer, pl.ds(rows - 2 * size, size)]
        else:
            depth = 2 * levels - stage
            bit = order[depth - 1]
            part = pl.ds(region(chunk, depth), rows >> depth)
            src = dst = res.at[layer, part]
        index = chunk * 2 * levels + stage
        return pltpu.make_async_remote_copy(
            src_ref=src, dst_ref=dst,
            send_sem=row_send.at[index], recv_sem=row_recv.at[index],
            device_id={"row": row_peer[bit]}, device_id_type=MESH,
        )

    def step(last):
        if last:
            wdl[...] = wd[...]
            wul[...] = wu[...]
            start(range(first))
        x1[...] = forward(0, x0_ref[...], x0_ref[...].astype(jnp.float32))
        outcome = forward(
            1, x1[...], x1[...].astype(jnp.float32), (lambda: advance(0)) if last else None
        )
        gr[...] = outcome.astype(jnp.float32) - tg_ref[...].astype(jnp.float32)

        def first_work():
            update_up(1, last)
            if last:
                advance(1)

        partial_act = dot_nt(gr[...].astype(jnp.bfloat16), wu[1]) * r_scale
        exchange(0, partial_act, None, first_work)
        row_dot = low_grads(1)
        through = dot_nt(low[...], wd[1]) * d_scale
        coefficient = row_dot * inv[1] * inv[1] / full
        gr[...] = gr[...] + through - coefficient * x1[...].astype(jnp.float32)

        def work():
            update(wd, md, 1, dot_nn(x1[...].T, low[...]) * d_scale, last)
            update_up(0, last)
            if last:
                mul[...] = mu[...].astype(jnp.bfloat16)
                mdl[1] = md[1].astype(jnp.bfloat16)
                start(range(first, len(chunks) - 1))
                advance(2)

        partial_act = dot_nt(gr[...].astype(jnp.bfloat16), wu[0]) * r_scale
        exchange(1, partial_act, None, work)
        low_grads(0)
        update(wd, md, 0, dot_nn(xt[...], low[...]) * d_scale, last)

    def middle(index, carry):
        step(False)
        return carry

    xt[...] = x0_ref[...].T
    lax.fori_loop(0, STEPS - 1, middle, 0)
    step(True)
    mdl[0] = md[0].astype(jnp.bfloat16)
    if not levels:
        wd_out[...] = wd[...]
        wu_out[...] = wu[...]
        md_out[...] = mdl[...]
        mu_out[...] = mul[...]
        return
    start([len(chunks) - 1])
    for slot in range(3, len(chunks) + 2 * levels - 1):
        advance(slot)
    for chunk in range(len(chunks)):
        for stage in range(2 * levels):
            row_copy(chunk, stage).wait_send()

    def stepped(weights, moments):
        moved = weights.astype(jnp.float32) - learn_rate * moments.astype(jnp.float32)
        return moved.astype(jnp.bfloat16)

    wd_out[...] = stepped(res_wd[...], res_md[...])
    wu_out[...] = stepped(res_wu[...], res_mu[...])
    md_out[...] = res_md[...]
    mu_out[...] = res_mu[...]


def fused(shards, replicas, hidden, target, w_down, w_up, m_down, m_up):
    tok, width = hidden.shape
    layers, _, rank = w_down.shape
    half = tok // 2
    hops = shards // 2 - 1
    bf, f32 = jnp.bfloat16, jnp.float32
    vmem = pl.BlockSpec(memory_space=pltpu.VMEM)
    sems = 2 + 2 * hops
    row_sems = max(1, 4 * layers * 2 * len(row_bits(replicas, width, rank)))
    return pl.pallas_call(
        functools.partial(fused_kernel, shards, replicas),
        out_shape=[
            jax.ShapeDtypeStruct(w_down.shape, bf),
            jax.ShapeDtypeStruct(w_up.shape, bf),
            jax.ShapeDtypeStruct(m_down.shape, bf),
            jax.ShapeDtypeStruct(m_up.shape, bf),
        ],
        in_specs=[vmem] * 6,
        out_specs=[vmem] * 4,
        scratch_shapes=[
            pltpu.VMEM(w_down.shape, bf),
            pltpu.VMEM(w_up.shape, bf),
            pltpu.VMEM(m_down.shape, f32),
            pltpu.VMEM(m_up.shape, f32),
            pltpu.VMEM(w_down.shape, bf),
            pltpu.VMEM(w_up.shape, bf),
            pltpu.VMEM(m_down.shape, bf),
            pltpu.VMEM(m_up.shape, bf),
            pltpu.VMEM(w_down.shape, bf),
            pltpu.VMEM(w_up.shape, bf),
            pltpu.VMEM(m_down.shape, bf),
            pltpu.VMEM(m_up.shape, bf),
            pltpu.VMEM(w_down.shape, bf),
            pltpu.VMEM(w_up.shape, bf),
            pltpu.VMEM(m_down.shape, bf),
            pltpu.VMEM(m_up.shape, bf),
            pltpu.SemaphoreType.DMA((row_sems,)),
            pltpu.SemaphoreType.DMA((row_sems,)),
            pltpu.VMEM((tok, width), bf),
            pltpu.VMEM((width, tok), bf),
            pltpu.VMEM((tok, width), f32),
            pltpu.VMEM((layers, tok, rank), f32),
            pltpu.VMEM((layers, tok, rank), bf),
            pltpu.VMEM((layers, tok, 1), f32),
            pltpu.VMEM((tok, rank), f32),
            pltpu.VMEM((tok, 1), f32),
            pltpu.VMEM((tok, rank), bf),
            pltpu.VMEM((half, rank), bf),
            pltpu.VMEM((half, rank), bf),
            pltpu.VMEM((half, rank), bf),
            pltpu.VMEM((2 * hops, half, rank), bf),
            pltpu.VMEM((half, rank), bf),
            pltpu.VMEM((half, rank), bf),
            pltpu.VMEM((8, half), f32),
            pltpu.VMEM((8, half), f32),
            pltpu.VMEM((8, half), f32),
            pltpu.VMEM((2 * hops, 8, half), f32),
            pltpu.VMEM((8, half), f32),
            pltpu.VMEM((8, half), f32),
            pltpu.SemaphoreType.DMA((sems,)),
            pltpu.SemaphoreType.DMA((sems,)),
            pltpu.SemaphoreType.DMA((sems,)),
            pltpu.SemaphoreType.DMA((sems,)),
        ],
        compiler_params=pltpu.CompilerParams(
            collective_id=0, has_side_effects=True, vmem_limit_bytes=60 * 1024 * 1024
        ),
    )(hidden, target, w_down, w_up, m_down, m_up)


def body(shards, replicas, hidden, target, w_down, w_up, m_down, m_up):
    means = fused(
        shards, replicas, hidden[0], target[0], w_down[0], w_up[0], m_down[0], m_up[0]
    )
    if not row_bits(replicas, hidden.shape[2], w_down.shape[3]):
        totals = lax.psum(tuple(means), "row")
        means = [total.astype(jnp.float32) / replicas for total in totals]
    return (
        means[0].astype(jnp.bfloat16),
        means[1].astype(jnp.bfloat16),
        means[2].astype(jnp.float32),
        means[3].astype(jnp.float32),
    )


def solution(mesh):
    placed = (
        P("row", None, "ta"),
        P("row", None, "ta"),
        P("row", None, "ta", None),
        P("row", None, None, "ta"),
        P("row", None, "ta", None),
        P("row", None, None, "ta"),
    )
    return jax.shard_map(
        functools.partial(body, mesh.shape["ta"], mesh.shape["row"]),
        mesh=mesh,
        in_specs=placed,
        out_specs=(
            P(None, "ta", None),
            P(None, None, "ta"),
            P(None, "ta", None),
            P(None, None, "ta"),
        ),
        check_vma=False,
    )
```

profile of v0, /device:TPU:0, one launch (start us, length us, event | category | flops | bytes accessed | tf_op | source)
XLA Modules:
  0.0 185.9 jit_solution(16541922913832497750)
XLA Ops:
  0.6 179.2 %shard_map.93 = (bf16[2,896,256]{2,1,0:T(8,128)(2,1)}, bf16[2,256,896]{2,1,0:T(8,128)(2,1)}, bf16[2,896,256]{2,1,0:T(8,128)(2,1)}, bf16[2,256,896]{2,1,0:T(8,128)(2,1)}) custom-call(bf16[256,896]{1,0:T(8,128)(2,1)} %bitcast.10, bf16[256,896]{1,0:T(8,128)(2,1)} %bitcast.11, bf16[2,896,256]{2,1,0:T(8,128)(2,1)} %bitcast.8, bf16[2,256,896]{2,1,0:T(8,128)(2,1)} %bitcast.9, ...), custom_call_target="tpu_custom_call" | custom-call | tf_op jit(solution)/shard_map/pallas_call | solution.py:308
  179.9 0.0 copy-start.2
  179.9 2.6 %convert_element_type.6 = f32[2,896,256]{2,1,0:T(8,128)} convert(bf16[2,896,256]{2,1,0:T(8,128)(2,1)} %get-tuple-element.10) | non-fusion elementwise | flops 458752 | bytes 2752512 | tf_op jit(solution)/shard_map/convert_element_type | solution.py:379
  182.5 0.0 copy-done.2
  182.5 0.0 copy-start.1
  182.5 0.0 copy-start
  182.5 1.4 convert_element_type.7
  183.9 0.2 copy-done.1
  184.0 0.9 copy.12
  184.9 0.0 copy-done
  184.9 0.9 copy.13
Async XLA Ops:
  179.9 2.6 %copy-start.2 = (bf16[2,256,896]{2,1,0:T(8,128)(2,1)S(1)}, bf16[2,256,896]{2,1,0:T(8,128)(2,1)}, u32[]{:S(2)}) copy-start(bf16[2,256,896]{2,1,0:T(8,128)(2,1)} %get-tuple-element.11) | copy-start | bytes 2752516
  182.5 1.5 copy-start.1
  182.5 2.4 %copy-start = (bf16[2,256,896]{2,1,0:T(8,128)(2,1)S(1)}, bf16[2,256,896]{2,1,0:T(8,128)(2,1)}, u32[]{:S(2)}) copy-start(bf16[2,256,896]{2,1,0:T(8,128)(2,1)} %get-tuple-element.17) | copy-start | bytes 2752516
where the time goes:
time: 186 us
  Pallas kernels  179 us (96%)
  other arithmetic  3.98 us (2%)
  local copies, waits for them, and re-layouts  2.01 us (1%)
    pallas_call x1, Pallas kernels, fused(): pl.pallas_call(functools.partial(fused_kernel, shards, replicas), out_sha...  179 us

commit v1 on v0

--- a/solution.py
+++ b/solution.py
@@ -34,8 +34,8 @@
     wd_out, wu_out, md_out, mu_out,
     wd, wu, md, mu, wdl, wul, mdl, mul, res_wd, res_wu, res_md, res_mu,
     got_wd, got_wu, got_md, got_mu, row_send, row_recv,
-    x1, xt, gr, pre, act, inv, tot, sqs, low,
-    s1, r1, s2, r2, s3, r3, q1, p1, q2, p2, q3, p3,
+    x1, xt, gr, pre, act, inv, low, proj, slope, gram, sqs,
+    s1, r1, s2, r2, s3, r3, tot, q1, p1, q2, p2, q3, p3,
     main_send, main_recv, side_send, side_recv,
 ):
     tok, width = x0_ref.shape
@@ -47,6 +47,7 @@
     core = lax.rem(me, 2)
     sibling = me + 1 - 2 * core
     partners = [lax.rem(me + 2 * k, shards) for k in range(1, chips)]
+    hops = chips - 1
     d_scale = full ** (-0.5)
     r_scale = rank ** (-0.5)
 
@@ -67,9 +68,6 @@
     md[...] = md_in[...]
     mu[...] = mu_in[...]
 
-    mine = pl.ds(pl.multiple_of(core * half, half), half)
-    other = pl.ds(pl.multiple_of((1 - core) * half, half), half)
-
     def send(src, dst, sems, index, peer):
         copy = pltpu.make_async_remote_copy(
             src_ref=src, dst_ref=dst,
@@ -81,6 +79,7 @@
 
     main = (main_send, main_recv)
     side = (side_send, side_recv)
+    per_channel = 2 + 2 * hops
 
     def to_row(column):
         return jnp.broadcast_to(column, (half, half)).T[0:8]
@@ -88,65 +87,75 @@
     def to_column(row):
         return jnp.broadcast_to(row[0:1, :], (half, half)).T[:, 0:1]
 
-    def exchange(parity, value, squares, work):
-        tot[...] = value
-        s1[...] = tot[other, :].astype(jnp.bfloat16)
-        copies = [send(s1, r1, main, 0, sibling)]
-        if squares is not None:
-            sqs[...] = squares
-            q1[...] = to_row(sqs[other, :])
-            copies.append(send(q1, p1, side, 0, sibling))
-            own_row = to_row(sqs[mine, :])
-        for copy in copies:
-            copy.wait()
-        pair = tot[mine, :] + r1[...].astype(jnp.float32)
-        s2[...] = pair.astype(jnp.bfloat16)
-        base = parity * (chips - 1)
-        copies = [
-            send(s2, r2.at[base + k], main, 1 + base + k, peer) for k, peer in enumerate(partners)
-        ]
-        if squares is not None:
-            pair_row = own_row + p1[...]
-            q2[...] = pair_row
-            copies += [
-                send(q2, p2.at[base + k], side, 1 + base + k, peer)
-                for k, peer in enumerate(partners)
+    class Channel:
+        def __init__(self, which):
+            self.which = which
+            self.size = tot[which].shape[0] // 2
+            size = self.size
+            self.mine = pl.ds(pl.multiple_of(core * size, size), size)
+            self.other = pl.ds(pl.multiple_of((1 - core) * size, size), size)
+            self.base = which * per_channel
+
+        def begin(self, parity, value, squares=None):
+            c = self.which
+            self.parity = parity
+            self.squares = squares is not None
+            tot[c][...] = value
+            s1[c][...] = tot[c][self.other, :].astype(jnp.bfloat16)
+            self.copies = [send(s1[c], r1[c], main, self.base, sibling)]
+            if self.squares:
+                sqs[...] = squares
+                q1[...] = to_row(sqs[self.other, :])
+                self.copies.append(send(q1, p1, side, 0, sibling))
+
+        def cross(self):
+            c = self.which
+            for copy in self.copies:
+                copy.wait()
+            pair = tot[c][self.mine, :] + r1[c][...].astype(jnp.float32)
+            s2[c][...] = pair.astype(jnp.bfloat16)
+            spots = [self.parity * hops + k for k in range(hops)]
+            self.copies = [
+                send(s2[c], r2[c].at[spot], main, self.base + 2 + spot, peer)
+                for spot, peer in zip(spots, partners)
             ]
-        if work is not None:
-            work()
-        for copy in copies:
-            copy.wait()
-        total = pair
-        for k in range(chips - 1):
-            total = total + r2[base + k].astype(jnp.float32)
-        last = 1 + 2 * (chips - 1)
-        s3[...] = total.astype(jnp.bfloat16)
-        copies = [send(s3, r3, main, last, sibling)]
-        tot[mine, :] = total
-        if squares is not None:
-            row = pair_row
-            for k in range(chips - 1):
-                row = row + p2[base + k]
-            q3[...] = row
-            copies.append(send(q3, p3, side, last, sibling))
-            sqs[mine, :] = to_column(row)
-        for copy in copies:
-            copy.wait()
-        tot[other, :] = r3[...].astype(jnp.float32)
-        if squares is not None:
-            sqs[other, :] = to_column(p3[...])
-
-    def forward(layer, rows, wide_rows, work=None):
-        squares = jnp.sum(wide_rows * wide_rows, axis=1, keepdims=True)
-        exchange(layer, dot_nn(rows, wd[layer]) * d_scale, squares, work)
-        inverse = lax.rsqrt(sqs[...] / full + norm_eps)
-        preact = tot[...] * inverse
-        activation = (preact * jax.nn.sigmoid(preact)).astype(jnp.bfloat16)
-        inv[layer] = inverse
-        pre[layer] = preact
-        act[layer] = activation
-        lifted = dot_nn(activation, wu[layer]) * r_scale
-        return (wide_rows + lifted).astype(jnp.bfloat16)
+            tot[c][self.mine, :] = pair
+            if self.squares:
+                self.row = to_row(sqs[self.mine, :]) + p1[...]
+                q2[...] = self.row
+                self.copies += [
+                    send(q2, p2.at[spot], side, 2 + spot, peer)
+                    for spot, peer in zip(spots, partners)
+                ]
+
+        def back(self):
+            c = self.which
+            for copy in self.copies:
+                copy.wait()
+            total = tot[c][self.mine, :]
+            for k in range(hops):
+                total = total + r2[c][self.parity * hops + k].astype(jnp.float32)
+            s3[c][...] = total.astype(jnp.bfloat16)
+            self.copies = [send(s3[c], r3[c], main, self.base + 1, sibling)]
+            tot[c][self.mine, :] = total
+            if self.squares:
+                row = self.row
+                for k in range(hops):
+                    row = row + p2[self.parity * hops + k]
+                q3[...] = row
+                self.copies.append(send(q3, p3, side, 1, sibling))
+                sqs[self.mine, :] = to_column(row)
+
+        def end(self):
+            c = self.which
+            for copy in self.copies:
+                copy.wait()
+            tot[c][self.other, :] = r3[c][...].astype(jnp.float32)
+            if self.squares:
+                sqs[self.other, :] = to_column(p3[...])
+            return tot[c][...]
+
+    forth, own_act, low_act, cross_weight, low_input = [Channel(k) for k in range(5)]
 
     def update(w, m, layer, grad, last):
         moment = moment_decay * m[layer] + grad
@@ -158,11 +167,20 @@
     def update_up(layer, last):
         update(wu, mu, layer, dot_nn(act[layer].T, gr[...].astype(jnp.bfloat16)) * r_scale, last)
 
-    def low_grads(layer):
+    def update_down(layer, rows_t, last):
+        update(wd, md, layer, dot_nn(rows_t, low[layer]) * d_scale, last)
+
+    def activate(layer, preact):
+        activation = (preact * jax.nn.sigmoid(preact)).astype(jnp.bfloat16)
+        pre[layer] = preact
+        act[layer] = activation
+        return activation
+
+    def low_grads(layer, grad_act):
         preact = pre[layer]
         sig = jax.nn.sigmoid(preact)
-        grad_pre = tot[...] * (sig * (1.0 + preact * (1.0 - sig)))
-        low[...] = (grad_pre * inv[layer]).astype(jnp.bfloat16)
+        grad_pre = grad_act * (sig * (1.0 + preact * (1.0 - sig)))
+        low[layer] = (grad_pre * inv[layer]).astype(jnp.bfloat16)
         return jnp.sum(grad_pre * preact, axis=1, keepdims=True)
 
     down, up = (wdl, got_wd, res_wd), (wul, got_wu, res_wu)
@@ -228,51 +246,94 @@
             device_id={"row": row_peer[bit]}, device_id_type=MESH,
         )
 
-    def step(last):
+    def step(parity, last, deferred):
         if last:
-            wdl[...] = wd[...]
             wul[...] = wu[...]
-            start(range(first))
-        x1[...] = forward(0, x0_ref[...], x0_ref[...].astype(jnp.float32))
-        outcome = forward(
-            1, x1[...], x1[...].astype(jnp.float32), (lambda: advance(0)) if last else None
-        )
+            wdl[1] = wd[1]
+            start(range(first - 1))
+        activation = activate(0, proj[...] * inv[0])
+        lifted = dot_nn(activation, wu[0]) * r_scale
+        x1[...] = (x0_ref[...].astype(jnp.float32) + lifted).astype(jnp.bfloat16)
+        wide = x1[...].astype(jnp.float32)
+        squares = jnp.sum(wide * wide, axis=1, keepdims=True)
+        forth.begin(parity, dot_nn(x1[...], wd[1]) * d_scale, squares)
+        cross_weight.begin(parity, dot_nn(wu[0], wd[1]) * (r_scale * d_scale))
+        forth.cross()
+        low_input.begin(parity, dot_nt(x1[...], wu[0]) * r_scale)
+        cross_weight.cross()
+        low_input.cross()
+        deferred()
+        if last:
+            wdl[0] = wd[0]
+            start([first - 1])
+            advance(0)
+        forth.back()
+        forth.end()
+        inv[1] = lax.rsqrt(sqs[...] / full + norm_eps)
+        activation = activate(1, tot[0][...] * inv[1])
+        lifted = dot_nn(activation, wu[1]) * r_scale
+        outcome = (x1[...].astype(jnp.float32) + lifted).astype(jnp.bfloat16)
         gr[...] = outcome.astype(jnp.float32) - tg_ref[...].astype(jnp.float32)
-
-        def first_work():
-            update_up(1, last)
-            if last:
-                advance(1)
-
-        partial_act = dot_nt(gr[...].astype(jnp.bfloat16), wu[1]) * r_scale
-        exchange(0, partial_act, None, first_work)
-        row_dot = low_grads(1)
-        through = dot_nt(low[...], wd[1]) * d_scale
+        grad_low = gr[...].astype(jnp.bfloat16)
+        own_act.begin(parity, dot_nt(grad_low, wu[1]) * r_scale)
+        low_act.begin(parity, dot_nt(grad_low, wu[0]) * r_scale)
+        own_act.cross()
+        low_act.cross()
+        update_up(1, last)
+        cross_weight.back()
+        low_input.back()
+        if last:
+            advance(1)
+        own_act.back()
+        row_dot = low_grads(1, own_act.end())
         coefficient = row_dot * inv[1] * inv[1] / full
+        through = dot_nt(low[1], wd[1]) * d_scale
         gr[...] = gr[...] + through - coefficient * x1[...].astype(jnp.float32)
-
-        def work():
-            update(wd, md, 1, dot_nn(x1[...].T, low[...]) * d_scale, last)
-            update_up(0, last)
-            if last:
-                mul[...] = mu[...].astype(jnp.bfloat16)
-                mdl[1] = md[1].astype(jnp.bfloat16)
-                start(range(first, len(chunks) - 1))
-                advance(2)
-
-        partial_act = dot_nt(gr[...].astype(jnp.bfloat16), wu[0]) * r_scale
-        exchange(1, partial_act, None, work)
-        low_grads(0)
-        update(wd, md, 0, dot_nn(xt[...], low[...]) * d_scale, last)
+        low_act.back()
+        update_up(0, last)
+        update_down(1, x1[...].T, last)
+        weight = cross_weight.end().astype(jnp.bfloat16)
+        grad_act = dot_nt(low[1], weight) - coefficient * low_input.end()
+        low_grads(0, low_act.end() + grad_act)
+        if last:
+            return
+        slope[...] = moment_decay * slope[...] + dot_nn(gram[...], low[0]) * (d_scale * d_scale)
+        proj[...] = proj[...] - learn_rate * slope[...]
+
+    def late_down(last=False):
+        update_down(0, xt[...], last)
 
     def middle(index, carry):
-        step(False)
+        step(lax.rem(index, 2), False, lambda: pl.when(index > 0)(late_down))
         return carry
 
     xt[...] = x0_ref[...].T
+    wide_input = x0_ref[...].astype(jnp.float32)
+    squares = jnp.sum(wide_input * wide_input, axis=1, keepdims=True)
+    forth.begin(1, dot_nn(x0_ref[...], wd[0]) * d_scale, squares)
+    own_act.begin(1, dot_nn(x0_ref[...], md[0].astype(jnp.bfloat16)) * d_scale)
+    low_act.begin(1, dot_nn(x0_ref[...], xt[...]))
+    forth.cross()
+    own_act.cross()
+    low_act.cross()
+    forth.back()
+    own_act.back()
+    low_act.back()
+    proj[...] = forth.end()
+    inv[0] = lax.rsqrt(sqs[...] / full + norm_eps)
+    slope[...] = own_act.end()
+    gram[...] = low_act.end().astype(jnp.bfloat16)
     lax.fori_loop(0, STEPS - 1, middle, 0)
-    step(True)
+    step((STEPS - 1) % 2, True, late_down)
+    if levels:
+        mul[...] = mu[...].astype(jnp.bfloat16)
+        mdl[1] = md[1].astype(jnp.bfloat16)
+        start(range(first, len(chunks) - 1))
+    late_down(True)
     mdl[0] = md[0].astype(jnp.bfloat16)
+    if not levels:
+        mul[...] = mu[...].astype(jnp.bfloat16)
+        mdl[1] = md[1].astype(jnp.bfloat16)
     if not levels:
         wd_out[...] = wd[...]
         wu_out[...] = wu[...]
@@ -280,7 +341,7 @@
         mu_out[...] = mul[...]
         return
     start([len(chunks) - 1])
-    for slot in range(3, len(chunks) + 2 * levels - 1):
+    for slot in range(2, len(chunks) + 2 * levels - 1):
         advance(slot)
     for chunk in range(len(chunks)):
         for stage in range(2 * levels):
@@ -303,7 +364,12 @@
     hops = shards // 2 - 1
     bf, f32 = jnp.bfloat16, jnp.float32
     vmem = pl.BlockSpec(memory_space=pltpu.VMEM)
-    sems = 2 + 2 * hops
+    channels = 5
+    sems = channels * (2 + 2 * hops)
+    rows = [tok, tok, tok, rank, tok]
+    halves = [pltpu.VMEM((count // 2, rank), bf) for count in rows]
+    crossed = [pltpu.VMEM((2 * hops, count // 2, rank), bf) for count in rows]
+    totals = [pltpu.VMEM((count, rank), f32) for count in rows]
     row_sems = max(1, 4 * layers * 2 * len(row_bits(replicas, width, rank)))
     return pl.pallas_call(
         functools.partial(fused_kernel, shards, replicas),
@@ -340,15 +406,18 @@
             pltpu.VMEM((layers, tok, rank), f32),
             pltpu.VMEM((layers, tok, rank), bf),
             pltpu.VMEM((layers, tok, 1), f32),
+            pltpu.VMEM((layers, tok, rank), bf),
             pltpu.VMEM((tok, rank), f32),
+            pltpu.VMEM((tok, rank), f32),
+            pltpu.VMEM((tok, tok), bf),
             pltpu.VMEM((tok, 1), f32),
-            pltpu.VMEM((tok, rank), bf),
-            pltpu.VMEM((half, rank), bf),
-            pltpu.VMEM((half, rank), bf),
-            pltpu.VMEM((half, rank), bf),
-            pltpu.VMEM((2 * hops, half, rank), bf),
-            pltpu.VMEM((half, rank), bf),
-            pltpu.VMEM((half, rank), bf),
+            halves,
+            halves,
+            halves,
+            crossed,
+            halves,
+            halves,
+            totals,
             pltpu.VMEM((8, half), f32),
             pltpu.VMEM((8, half), f32),
             pltpu.VMEM((8, half), f32),
@@ -357,8 +426,8 @@
             pltpu.VMEM((8, half), f32),
             pltpu.SemaphoreType.DMA((sems,)),
             pltpu.SemaphoreType.DMA((sems,)),
-            pltpu.SemaphoreType.DMA((sems,)),
-            pltpu.SemaphoreType.DMA((sems,)),
+            pltpu.SemaphoreType.DMA((2 + 2 * hops,)),
+            pltpu.SemaphoreType.DMA((2 + 2 * hops,)),
         ],
         compiler_params=pltpu.CompilerParams(
             collective_id=0, has_side_effects=True, vmem_limit_bytes=60 * 1024 * 1024

time: 186 us -> 162 us (0.87)
  Pallas kernels: 179 us -> 153 us
    pallas_call x1, Pallas kernels: 179 us -> 153 us  [fused(): pl.pallas_call(functools.partial(fused_kernel, shards, replicas), out_sha...]
where the time goes in v1:
time: 162 us; the launch traced here: 160 us
  Pallas kernels  153 us (94%)
  other arithmetic  3.98 us (2%)
  local copies, waits for them, and re-layouts  2.01 us (1%)
    pallas_call x1, Pallas kernels, fused(): pl.pallas_call(functools.partial(fused_kernel, shards, replicas), out_sha...  153 us

profile of v1, /device:TPU:0, one launch (start us, length us, event | category | flops | bytes accessed | tf_op | source)
XLA Modules:
  0.0 160.1 jit_solution(4566502225322677680)
XLA Ops:
  0.6 153.5 %shard_map.93 = (bf16[2,896,256]{2,1,0:T(8,128)(2,1)}, bf16[2,256,896]{2,1,0:T(8,128)(2,1)}, bf16[2,896,256]{2,1,0:T(8,128)(2,1)}, bf16[2,256,896]{2,1,0:T(8,128)(2,1)}) custom-call(bf16[256,896]{1,0:T(8,128)(2,1)} %bitcast.10, bf16[256,896]{1,0:T(8,128)(2,1)} %bitcast.11, bf16[2,896,256]{2,1,0:T(8,128)(2,1)} %bitcast.8, bf16[2,256,896]{2,1,0:T(8,128)(2,1)} %bitcast.9, ...), custom_call_target="tpu_custom_call" | custom-call | tf_op jit(solution)/shard_map/pallas_call | solution.py:374
  154.1 0.0 copy-start.2
  154.1 2.6 %convert_element_type.6 = f32[2,896,256]{2,1,0:T(8,128)} convert(bf16[2,896,256]{2,1,0:T(8,128)(2,1)} %get-tuple-element.10) | non-fusion elementwise | flops 458752 | bytes 2752512 | tf_op jit(solution)/shard_map/convert_element_type | solution.py:448
  156.7 0.0 copy-done.2
  156.7 0.0 copy-start.1
  156.7 0.0 copy-start
  156.7 1.4 convert_element_type.7
  158.1 0.2 copy-done.1
  158.2 0.9 copy.12
  159.2 0.0 copy-done
  159.2 0.9 copy.13
Async XLA Ops:
  154.1 2.6 %copy-start.2 = (bf16[2,256,896]{2,1,0:T(8,128)(2,1)S(1)}, bf16[2,256,896]{2,1,0:T(8,128)(2,1)}, u32[]{:S(2)}) copy-start(bf16[2,256,896]{2,1,0:T(8,128)(2,1)} %get-tuple-element.11) | copy-start | bytes 2752516
  156.7 1.5 copy-start.1
  156.7 2.4 %copy-start = (bf16[2,256,896]{2,1,0:T(8,128)(2,1)S(1)}, bf16[2,256,896]{2,1,0:T(8,128)(2,1)}, u32[]{:S(2)}) copy-start(bf16[2,256,896]{2,1,0:T(8,128)(2,1)} %get-tuple-element.17) | copy-start | bytes 2752516

commit v2 on v1

--- a/solution.py
+++ b/solution.py
@@ -22,10 +22,20 @@
     return lax.dot_general(a, b, (((1,), (1,)), ((), ())), preferred_element_type=jnp.float32)
 
 
-def row_bits(replicas, *lengths):
-    if replicas & (replicas - 1) or any(length % (16 * replicas) for length in lengths):
-        return []
-    return [2**k for k in range(replicas.bit_length() - 1)]
+LINES = 4
+FOLD_PARTS, LINE_PARTS = 5, 2
+KINDS = 6
+
+
+def on_grid(replicas, width, rank):
+    return replicas == 2 * LINES and width % 128 == 0 and rank % 128 == 0 and width >= 512
+
+
+def cuts(length, wide):
+    if not wide:
+        return [("fold", k * (length // 2), length // 2) for k in range(2)]
+    line = length * LINE_PARTS // (FOLD_PARTS + LINE_PARTS) // 128 * 128
+    return [("line", 0, line), ("fold", line, length - line)]
 
 
 def fused_kernel(
@@ -54,14 +64,15 @@
     barrier = pltpu.get_barrier_semaphore()
     for peer in [sibling] + partners:
         pl.semaphore_signal(barrier, inc=1, device_id={"ta": peer}, device_id_type=MESH)
-    bits = row_bits(replicas, width, rank)
-    levels = len(bits)
+    levels = on_grid(replicas, width, rank)
     spot = lax.axis_index("row")
-    own_bit = {bit: lax.rem(spot // bit, 2) for bit in bits}
-    row_peer = {bit: spot + bit - 2 * bit * own_bit[bit] for bit in bits}
-    for bit in bits:
-        pl.semaphore_signal(barrier, inc=1, device_id={"row": row_peer[bit]}, device_id_type=MESH)
-    pl.semaphore_wait(barrier, chips + levels)
+    line, side_of = spot // 2, lax.rem(spot, 2)
+    facing = spot + 1 - 2 * side_of
+    after, before = lax.rem(spot + 2, replicas), lax.rem(spot + replicas - 2, replicas)
+    greeted = [facing, after, before] if levels else []
+    for peer in greeted:
+        pl.semaphore_signal(barrier, inc=1, device_id={"row": peer}, device_id_type=MESH)
+    pl.semaphore_wait(barrier, chips + len(greeted))
 
     wd[...] = wd_in[...]
     wu[...] = wu_in[...]
@@ -186,71 +197,207 @@
     down, up = (wdl, got_wd, res_wd), (wul, got_wu, res_wu)
     mdown, mup = (mdl, got_md, res_md), (mul, got_mu, res_mu)
     layers = list(reversed(range(wd.shape[0])))
-    chunks = [pair + (layer, bits) for layer in layers for pair in (up, down)]
-    first = len(chunks)
-    swapped = bits[:2][::-1] + bits[2:]
-    chunks += [
-        pair + (layer, swapped if layer == 0 and pair is mup else bits)
-        for layer in layers
-        for pair in (mup, mdown)
-    ]
+    chunks = []
+    for pairs in ((up, down), (mup, mdown)):
+        for layer in layers:
+            for pair, wide in zip(pairs, (False, True)):
+                for form, base, size in cuts(pair[0].shape[1], wide):
+                    chunks.append((pair, layer, form, base, size))
+    first = len(chunks) // 2
+    part = first // 4
+    sent = []
+
+    class Piece:
+        def __init__(self, index):
+            (self.acc, self.got, self.res), self.layer, self.form, self.base, self.size = chunks[index]
+            self.index = index
+            self.stages = 7 if self.form == "fold" else 9
+
+        def rows(self, ref, start, size, slot=0):
+            first_row = self.base + (slot - 1 if slot else 0) * self.acc.shape[1]
+            start = start + first_row
+            if not isinstance(start, int):
+                start = pl.multiple_of(start, 16)
+            return ref.at[self.layer, pl.ds(start, size)]
+
+        def copy(self, kind, src, dst, peer):
+            index = self.index * KINDS + kind
+            return pltpu.make_async_remote_copy(
+                src_ref=src, dst_ref=dst,
+                send_sem=row_send.at[index], recv_sem=row_recv.at[index],
+                device_id={"row": peer}, device_id_type=MESH,
+            )
+
+        def sum_out(self, kind, start, size, slot, landing, peer, when=None):
+            def go(finish=False):
+                made = self.copy(
+                    kind, self.rows(self.acc, start, size), self.rows(self.got, landing, size, slot), peer
+                )
+                made.wait_send() if finish else made.start()
+
+            go()
+            sent.append((when, functools.partial(go, True)))
+
+        def mean_out(self, kind, start, size, peer, when=None):
+            def go(finish=False):
+                where = self.rows(self.res, start, size)
+                made = self.copy(kind, where, where, peer)
+                made.wait_send() if finish else made.start()
+
+            go()
+            sent.append((when, functools.partial(go, True)))
+
+        def landed(self, kind, start, size, slot=0):
+            ref = self.rows(self.got, start, size, slot) if slot else self.rows(self.res, start, size)
+            self.copy(kind, ref, ref, facing).wait_recv()
+
+        def add(self, start, size, slot, landing):
+            mine = self.rows(self.acc, start, size)
+            came = self.rows(self.got, landing, size, slot)
+            total = mine[...].astype(jnp.float32) + came[...].astype(jnp.float32)
+            mine[...] = total.astype(jnp.bfloat16)
+
+        def settle(self, start, size, slot, landing):
+            mine = self.rows(self.acc, start, size)
+            came = self.rows(self.got, landing, size, slot)
+            total = mine[...].astype(jnp.float32) + came[...].astype(jnp.float32)
+            self.rows(self.res, start, size)[...] = (total * (1.0 / replicas)).astype(jnp.bfloat16)
+
+        def run(self, stage):
+            (self.fold if self.form == "fold" else self.line)(stage)
+
+        def fold(self, stage):
+            half_size, quarter = self.size // 2, self.size // 4
+            keep, away = side_of * half_size, (1 - side_of) * half_size
+            outer = (line == 0) | (line == LINES - 1)
+            inner = jnp.logical_not(outer)
+            upper = lax.rem(line // 2, 2)
+            inward = spot + 2 - 4 * upper
+            outward = spot - 2 + 4 * upper
+            across = spot + 2 - 4 * upper
+            own = keep + upper * quarter
+            far = keep + (1 - upper) * quarter
+            if stage == 0:
+                self.sum_out(0, away, half_size, 1, 0, facing)
+            elif stage == 1:
+                self.landed(0, 0, half_size, 1)
+                self.add(keep, half_size, 1, 0)
+
+                @pl.when(outer)
+                def _():
+                    self.sum_out(1, keep, half_size, 2, 0, inward, outer)
+            elif stage == 2:
+
+                @pl.when(inner)
+                def _():
+                    self.landed(1, 0, half_size, 2)
+                    self.add(keep, half_size, 2, 0)
+                    self.sum_out(2, far, quarter, 3, 0, across, inner)
+            elif stage == 3:
+
+                @pl.when(inner)
+                def _():
+                    self.landed(2, 0, quarter, 3)
+                    self.settle(own, quarter, 3, 0)
+                    self.mean_out(3, own, quarter, across, inner)
+            elif stage == 4:
+
+                @pl.when(inner)
+                def _():
+                    self.landed(3, far, quarter)
+                    self.mean_out(4, keep, half_size, outward, inner)
+                    self.mean_out(5, keep, half_size, facing, inner)
+            elif stage == 5:
+
+                @pl.when(outer)
+                def _():
+                    self.landed(4, keep, half_size)
+                    self.mean_out(5, keep, half_size, facing, outer)
+            else:
+                self.landed(5, away, half_size)
+
+        def line(self, stage):
+            piece = self.size // LINES
+            fine = piece // 2
+            end = LINES - 1
+            if stage <= end:
+                for at, step_to, kind, slot in ((stage, 1, 0, 1), (end - stage, -1, 1, 2)):
+                    ahead = (at + 1) * piece if step_to > 0 else 0
+                    count = (end - at) * piece if step_to > 0 else at * piece
+                    came = (LINES - at) * piece if step_to > 0 else (at + 1) * piece
+                    opened = at * piece if step_to > 0 else 0
+                    here = line == at
+
+                    @pl.when(here)
+                    def _(ahead=ahead, count=count, came=came, opened=opened, kind=kind, slot=slot, here=here, peer=after if step_to > 0 else before):
+                        if stage:
+                            self.landed(kind, opened, came, slot)
+                        if count:
+                            if stage:
+                                self.add(ahead, count, slot, ahead)
+                            self.sum_out(kind, ahead, count, slot, ahead, peer, here)
+            if stage == end:
+                own = line * piece
+
+                @pl.when(line > 0)
+                def _():
+                    self.add(own, piece, 1, own)
+
+                @pl.when(line < end)
+                def _():
+                    self.add(own, piece, 2, own)
+
+                self.sum_out(2, own + (1 - side_of) * fine, fine, 3, 0, facing)
+            elif stage == end + 1:
+                own = line * piece + side_of * fine
+                self.landed(2, 0, fine, 3)
+                self.settle(own, fine, 3, 0)
+                self.mean_out(3, own, fine, facing)
+            elif stage > end + 1:
+                hop = stage - end - 2
+                if hop == 0:
+                    self.landed(3, line * piece + (1 - side_of) * fine, fine)
+                for at, step_to, kind in ((hop, 1, 4), (end - hop, -1, 5)):
+                    here = line == at
+                    came = hop * piece
+                    opened = 0 if step_to > 0 else (at + 1) * piece
+                    begun = 0 if step_to > 0 else at * piece
+
+                    @pl.when(here)
+                    def _(came=came, opened=opened, begun=begun, kind=kind, here=here, peer=after if step_to > 0 else before):
+                        if hop:
+                            self.landed(kind, opened, came)
+                        if hop < end:
+                            self.mean_out(kind, begun, came + piece, peer, here)
+
+    pieces = [Piece(k) for k in range(len(chunks))] if levels else []
+    done = {k: 0 for k in range(len(chunks))}
+    plan = sorted(
+        (0.25 * (k % first) + (2.0 if k >= first else 0.0) + stage, k, stage)
+        for k, piece in enumerate(pieces)
+        for stage in range(1, piece.stages)
+    )
 
     def start(picked):
-        for chunk in picked if levels else []:
-            row_copy(chunk, 0).start()
-
-    def advance(slot):
-        for chunk in range(len(chunks)):
-            stage = slot - chunk
-            if not levels or stage < 0 or stage >= 2 * levels:
+        for k in picked if levels else []:
+            pieces[k].run(0)
+
+    def advance(count=None, below=None):
+        taken = 0
+        for entry in list(plan):
+            if taken == count:
+                break
+            if below is not None and entry[1] >= below:
                 continue
-            row_copy(chunk, stage).wait_recv()
-            if stage < levels:
-                acc, got, res, layer, order = chunks[chunk]
-                size = acc.shape[1] >> (stage + 1)
-                keep = pl.ds(region(chunk, stage + 1), size)
-                landed = got.at[layer, pl.ds(acc.shape[1] - 2 * size, size)]
-                total = acc[layer, keep, :].astype(jnp.float32) + landed[...].astype(jnp.float32)
-                if stage < levels - 1:
-                    acc[layer, keep, :] = total.astype(jnp.bfloat16)
-                else:
-                    res[layer, keep, :] = (total * (1.0 / replicas)).astype(jnp.bfloat16)
-            if stage < 2 * levels - 1:
-                row_copy(chunk, stage + 1).start()
-
-    def region(chunk, depth):
-        acc, _, _, _, order = chunks[chunk]
-        start = 0
-        for k in range(depth):
-            start = start + own_bit[order[k]] * (acc.shape[1] >> (k + 1))
-        return pl.multiple_of(start, acc.shape[1] >> depth) if depth else 0
-
-    def row_copy(chunk, stage):
-        acc, got, res, layer, order = chunks[chunk]
-        rows = acc.shape[1]
-        if stage < levels:
-            bit = order[stage]
-            size = rows >> (stage + 1)
-            away = region(chunk, stage) + (1 - own_bit[bit]) * size
-            src = acc.at[layer, pl.ds(pl.multiple_of(away, size), size)]
-            dst = got.at[layer, pl.ds(rows - 2 * size, size)]
-        else:
-            depth = 2 * levels - stage
-            bit = order[depth - 1]
-            part = pl.ds(region(chunk, depth), rows >> depth)
-            src = dst = res.at[layer, part]
-        index = chunk * 2 * levels + stage
-        return pltpu.make_async_remote_copy(
-            src_ref=src, dst_ref=dst,
-            send_sem=row_send.at[index], recv_sem=row_recv.at[index],
-            device_id={"row": row_peer[bit]}, device_id_type=MESH,
-        )
+            pieces[entry[1]].run(entry[2])
+            plan.remove(entry)
+            taken += 1
 
     def step(parity, last, deferred):
         if last:
             wul[...] = wu[...]
             wdl[1] = wd[1]
-            start(range(first - 1))
+            start(range(first - part))
         activation = activate(0, proj[...] * inv[0])
         lifted = dot_nn(activation, wu[0]) * r_scale
         x1[...] = (x0_ref[...].astype(jnp.float32) + lifted).astype(jnp.bfloat16)
@@ -265,8 +412,8 @@
         deferred()
         if last:
             wdl[0] = wd[0]
-            start([first - 1])
-            advance(0)
+            start(range(first - part, first))
+            advance(4, first)
         forth.back()
         forth.end()
         inv[1] = lax.rsqrt(sqs[...] / full + norm_eps)
@@ -283,7 +430,7 @@
         cross_weight.back()
         low_input.back()
         if last:
-            advance(1)
+            advance(6, first)
         own_act.back()
         row_dot = low_grads(1, own_act.end())
         coefficient = row_dot * inv[1] * inv[1] / full
@@ -328,7 +475,7 @@
     if levels:
         mul[...] = mu[...].astype(jnp.bfloat16)
         mdl[1] = md[1].astype(jnp.bfloat16)
-        start(range(first, len(chunks) - 1))
+        start(range(first, len(chunks) - part))
     late_down(True)
     mdl[0] = md[0].astype(jnp.bfloat16)
     if not levels:
@@ -340,12 +487,13 @@
         md_out[...] = mdl[...]
         mu_out[...] = mul[...]
         return
-    start([len(chunks) - 1])
-    for slot in range(2, len(chunks) + 2 * levels - 1):
-        advance(slot)
-    for chunk in range(len(chunks)):
-        for stage in range(2 * levels):
-            row_copy(chunk, stage).wait_send()
+    start(range(len(chunks) - part, len(chunks)))
+    advance()
+    for when, finish in sent:
+        if when is None:
+            finish()
+        else:
+            pl.when(when)(finish)
 
     def stepped(weights, moments):
         moved = weights.astype(jnp.float32) - learn_rate * moments.astype(jnp.float32)
@@ -370,7 +518,8 @@
     halves = [pltpu.VMEM((count // 2, rank), bf) for count in rows]
     crossed = [pltpu.VMEM((2 * hops, count // 2, rank), bf) for count in rows]
     totals = [pltpu.VMEM((count, rank), f32) for count in rows]
-    row_sems = max(1, 4 * layers * 2 * len(row_bits(replicas, width, rank)))
+    row_sems = 8 * layers * KINDS
+    tripled = [(layers, 3 * count, other) for count, other in (w_down.shape[1:], w_up.shape[1:])] * 2
     return pl.pallas_call(
         functools.partial(fused_kernel, shards, replicas),
         out_shape=[
@@ -394,10 +543,10 @@
             pltpu.VMEM(w_up.shape, bf),
             pltpu.VMEM(m_down.shape, bf),
             pltpu.VMEM(m_up.shape, bf),
-            pltpu.VMEM(w_down.shape, bf),
-            pltpu.VMEM(w_up.shape, bf),
-            pltpu.VMEM(m_down.shape, bf),
-            pltpu.VMEM(m_up.shape, bf),
+            pltpu.VMEM(tripled[0], bf),
+            pltpu.VMEM(tripled[1], bf),
+            pltpu.VMEM(tripled[2], bf),
+            pltpu.VMEM(tripled[3], bf),
             pltpu.SemaphoreType.DMA((row_sems,)),
             pltpu.SemaphoreType.DMA((row_sems,)),
             pltpu.VMEM((tok, width), bf),
@@ -439,7 +588,7 @@
     means = fused(
         shards, replicas, hidden[0], target[0], w_down[0], w_up[0], m_down[0], m_up[0]
     )
-    if not row_bits(replicas, hidden.shape[2], w_down.shape[3]):
+    if not on_grid(replicas, hidden.shape[2], w_down.shape[3]):
         totals = lax.psum(tuple(means), "row")
         means = [total.astype(jnp.float32) / replicas for total in totals]
     return (

time: 162 us -> 155 us (0.957)
  Pallas kernels: 153 us -> 148 us
    pallas_call x1, Pallas kernels: 153 us -> 148 us  [fused(): pl.pallas_call(functools.partial(fused_kernel, shards, replicas), out_sha...]
where the time goes in v2:
time: 155 us; the launch traced here: 154 us
  Pallas kernels  148 us (95%)
  other arithmetic  3.98 us (3%)
  local copies, waits for them, and re-layouts  2.01 us (1%)
    pallas_call x1, Pallas kernels, fused(): pl.pallas_call(functools.partial(fused_kernel, shards, replicas), out_sha...  148 us

profile of v2, /device:TPU:0, one launch (start us, length us, event | category | flops | bytes accessed | tf_op | source)
XLA Modules:
  0.0 154.5 jit_solution(1101831162160832490)
XLA Ops:
  0.6 147.8 %shard_map.93 = (bf16[2,896,256]{2,1,0:T(8,128)(2,1)}, bf16[2,256,896]{2,1,0:T(8,128)(2,1)}, bf16[2,896,256]{2,1,0:T(8,128)(2,1)}, bf16[2,256,896]{2,1,0:T(8,128)(2,1)}) custom-call(bf16[256,896]{1,0:T(8,128)(2,1)} %bitcast.10, bf16[256,896]{1,0:T(8,128)(2,1)} %bitcast.11, bf16[2,896,256]{2,1,0:T(8,128)(2,1)} %bitcast.8, bf16[2,256,896]{2,1,0:T(8,128)(2,1)} %bitcast.9, ...), custom_call_target="tpu_custom_call" | custom-call | tf_op jit(solution)/shard_map/pallas_call | solution.py:523
  148.5 0.0 copy-start.2
  148.5 2.6 %convert_element_type.6 = f32[2,896,256]{2,1,0:T(8,128)} convert(bf16[2,896,256]{2,1,0:T(8,128)(2,1)} %get-tuple-element.10) | non-fusion elementwise | flops 458752 | bytes 2752512 | tf_op jit(solution)/shard_map/convert_element_type | solution.py:597
  151.1 0.0 copy-done.2
  151.1 0.0 copy-start.1
  151.1 0.0 copy-start
  151.1 1.4 convert_element_type.7
  152.5 0.2 copy-done.1
  152.6 0.9 copy.12
  153.5 0.0 copy-done
  153.5 0.9 copy.13
Async XLA Ops:
  148.5 2.6 %copy-start.2 = (bf16[2,256,896]{2,1,0:T(8,128)(2,1)S(1)}, bf16[2,256,896]{2,1,0:T(8,128)(2,1)}, u32[]{:S(2)}) copy-start(bf16[2,256,896]{2,1,0:T(8,128)(2,1)} %get-tuple-element.11) | copy-start | bytes 2752516
  151.1 1.5 copy-start.1
  151.1 2.4 %copy-start = (bf16[2,256,896]{2,1,0:T(8,128)(2,1)S(1)}, bf16[2,256,896]{2,1,0:T(8,128)(2,1)}, u32[]{:S(2)}) copy-start(bf16[2,256,896]{2,1,0:T(8,128)(2,1)} %get-tuple-element.17) | copy-start | bytes 2752516

commit v3 on v2

--- a/solution.py
+++ b/solution.py
@@ -40,16 +40,24 @@
 
 def fused_kernel(
     shards, replicas,
-    x0_ref, tg_ref, wd_in, wu_in, md_in, mu_in,
+    x0_in, tg_in, wd_in, wu_in, md_in, mu_in,
     wd_out, wu_out, md_out, mu_out,
-    wd, wu, md, mu, wdl, wul, mdl, mul, res_wd, res_wu, res_md, res_mu,
+    x0_ref, tg_ref, wd, wu, md, mu, load_sem, store_sem, wdl, wul, mdl, mul, res_wd, res_wu, res_md, res_mu,
     got_wd, got_wu, got_md, got_mu, row_send, row_recv,
-    x1, xt, gr, pre, act, inv, low, proj, slope, gram, sqs,
+    x1, x1t, xt, gr, pre, act, inv, low, proj, slope, gram, sqs,
     s1, r1, s2, r2, s3, r3, tot, q1, p1, q2, p2, q3, p3,
     main_send, main_recv, side_send, side_recv,
 ):
     tok, width = x0_ref.shape
     rank = wd.shape[2]
+    loads = [
+        pltpu.make_async_copy(source, target, load_sem.at[k])
+        for k, (source, target) in enumerate((
+            (x0_in, x0_ref), (wd_in, wd), (md_in, md), (wu_in, wu), (tg_in, tg_ref), (mu_in, mu),
+        ))
+    ]
+    for load in loads:
+        load.start()
     full = width * shards
     half = tok // 2
     chips = shards // 2
@@ -73,11 +81,6 @@
     for peer in greeted:
         pl.semaphore_signal(barrier, inc=1, device_id={"row": peer}, device_id_type=MESH)
     pl.semaphore_wait(barrier, chips + len(greeted))
-
-    wd[...] = wd_in[...]
-    wu[...] = wu_in[...]
-    md[...] = md_in[...]
-    mu[...] = mu_in[...]
 
     def send(src, dst, sems, index, peer):
         copy = pltpu.make_async_remote_copy(
@@ -166,7 +169,9 @@
                 sqs[self.other, :] = to_column(p3[...])
             return tot[c][...]
 
-    forth, own_act, low_act, cross_weight, low_input = [Channel(k) for k in range(5)]
+    forth, own_act, low_act, cross_weight, low_input, first_slope, first_gram = [
+        Channel(k) for k in range(7)
+    ]
 
     def update(w, m, layer, grad, last):
         moment = moment_decay * m[layer] + grad
@@ -409,6 +414,7 @@
         low_input.begin(parity, dot_nt(x1[...], wu[0]) * r_scale)
         cross_weight.cross()
         low_input.cross()
+        x1t[...] = x1[...].T
         deferred()
         if last:
             wdl[0] = wd[0]
@@ -438,7 +444,7 @@
         gr[...] = gr[...] + through - coefficient * x1[...].astype(jnp.float32)
         low_act.back()
         update_up(0, last)
-        update_down(1, x1[...].T, last)
+        update_down(1, x1t[...], last)
         weight = cross_weight.end().astype(jnp.bfloat16)
         grad_act = dot_nt(low[1], weight) - coefficient * low_input.end()
         low_grads(0, low_act.end() + grad_act)
@@ -450,26 +456,37 @@
     def late_down(last=False):
         update_down(0, xt[...], last)
 
+    def carried():
+        first_slope.back()
+        first_gram.back()
+        slope[...] = first_slope.end()
+        gram[...] = first_gram.end().astype(jnp.bfloat16)
+
     def middle(index, carry):
-        step(lax.rem(index, 2), False, lambda: pl.when(index > 0)(late_down))
+        def deferred():
+            pl.when(index == 0)(carried)
+            pl.when(index > 0)(late_down)
+
+        step(lax.rem(index, 2), False, deferred)
         return carry
 
+    loads[0].wait()
     xt[...] = x0_ref[...].T
     wide_input = x0_ref[...].astype(jnp.float32)
     squares = jnp.sum(wide_input * wide_input, axis=1, keepdims=True)
+    loads[1].wait()
     forth.begin(1, dot_nn(x0_ref[...], wd[0]) * d_scale, squares)
-    own_act.begin(1, dot_nn(x0_ref[...], md[0].astype(jnp.bfloat16)) * d_scale)
-    low_act.begin(1, dot_nn(x0_ref[...], xt[...]))
+    loads[2].wait()
+    first_slope.begin(1, dot_nn(x0_ref[...], md[0].astype(jnp.bfloat16)) * d_scale)
+    first_gram.begin(1, dot_nn(x0_ref[...], xt[...]))
     forth.cross()
-    own_act.cross()
-    low_act.cross()
+    first_slope.cross()
+    first_gram.cross()
+    for load in loads[3:]:
+        load.wait()
     forth.back()
-    own_act.back()
-    low_act.back()
     proj[...] = forth.end()
     inv[0] = lax.rsqrt(sqs[...] / full + norm_eps)
-    slope[...] = own_act.end()
-    gram[...] = low_act.end().astype(jnp.bfloat16)
     lax.fori_loop(0, STEPS - 1, middle, 0)
     step((STEPS - 1) % 2, True, late_down)
     if levels:
@@ -481,28 +498,56 @@
     if not levels:
         mul[...] = mu[...].astype(jnp.bfloat16)
         mdl[1] = md[1].astype(jnp.bfloat16)
+    outs = ((wd_out, res_wd, wd), (wu_out, res_wu, wu), (md_out, res_md, mdl), (mu_out, res_mu, mul))
     if not levels:
-        wd_out[...] = wd[...]
-        wu_out[...] = wu[...]
-        md_out[...] = mdl[...]
-        mu_out[...] = mul[...]
+        stores = [pltpu.make_async_copy(kept, out, store_sem.at[k]) for k, (out, _, kept) in enumerate(outs)]
+        for store in stores:
+            store.start()
+        for store in stores:
+            store.wait()
         return
     start(range(len(chunks) - part, len(chunks)))
     advance()
+    stores = []
+    for piece in pieces:
+        for out, res, _ in outs:
+            if res is piece.res:
+                stores.append(pltpu.make_async_copy(
+                    piece.rows(res, 0, piece.size), piece.rows(out, 0, piece.size), store_sem.at[piece.index]
+                ))
+                stores[-1].start()
     for when, finish in sent:
         if when is None:
             finish()
         else:
             pl.when(when)(finish)
-
-    def stepped(weights, moments):
-        moved = weights.astype(jnp.float32) - learn_rate * moments.astype(jnp.float32)
-        return moved.astype(jnp.bfloat16)
-
-    wd_out[...] = stepped(res_wd[...], res_md[...])
-    wu_out[...] = stepped(res_wu[...], res_mu[...])
-    md_out[...] = res_md[...]
-    mu_out[...] = res_mu[...]
+    for store in stores:
+        store.wait()
+
+
+def finish_kernel(wd_ref, wu_ref, md_ref, mu_ref, wd_out, wu_out, md_out, mu_out):
+    for w_ref, m_ref, w_out, m_out in ((wd_ref, md_ref, wd_out, md_out), (wu_ref, mu_ref, wu_out, mu_out)):
+        moments = m_ref[...].astype(jnp.float32)
+        moved = w_ref[...].astype(jnp.float32) - learn_rate * moments
+        w_out[...] = moved.astype(jnp.bfloat16)
+        m_out[...] = moments
+
+
+def finish(means):
+    layers = means[0].shape[0]
+    parts = 2
+    specs = [
+        pl.BlockSpec((1, mean.shape[1] // parts, mean.shape[2]), lambda i: (i // parts, i % parts, 0))
+        for mean in means
+    ]
+    kinds = [jnp.bfloat16, jnp.bfloat16, jnp.float32, jnp.float32]
+    return pl.pallas_call(
+        finish_kernel,
+        grid=(layers * parts,),
+        out_shape=[jax.ShapeDtypeStruct(mean.shape, kind) for mean, kind in zip(means, kinds)],
+        in_specs=specs,
+        out_specs=specs,
+    )(*means)
 
 
 def fused(shards, replicas, hidden, target, w_down, w_up, m_down, m_up):
@@ -511,10 +556,10 @@
     half = tok // 2
     hops = shards // 2 - 1
     bf, f32 = jnp.bfloat16, jnp.float32
-    vmem = pl.BlockSpec(memory_space=pltpu.VMEM)
-    channels = 5
+    hbm = pl.BlockSpec(memory_space=pl.ANY)
+    channels = 7
     sems = channels * (2 + 2 * hops)
-    rows = [tok, tok, tok, rank, tok]
+    rows = [tok, tok, tok, rank, tok, tok, tok]
     halves = [pltpu.VMEM((count // 2, rank), bf) for count in rows]
     crossed = [pltpu.VMEM((2 * hops, count // 2, rank), bf) for count in rows]
     totals = [pltpu.VMEM((count, rank), f32) for count in rows]
@@ -528,13 +573,17 @@
             jax.ShapeDtypeStruct(m_down.shape, bf),
             jax.ShapeDtypeStruct(m_up.shape, bf),
         ],
-        in_specs=[vmem] * 6,
-        out_specs=[vmem] * 4,
+        in_specs=[hbm] * 6,
+        out_specs=[hbm] * 4,
         scratch_shapes=[
+            pltpu.VMEM(hidden.shape, bf),
+            pltpu.VMEM(target.shape, bf),
             pltpu.VMEM(w_down.shape, bf),
             pltpu.VMEM(w_up.shape, bf),
             pltpu.VMEM(m_down.shape, f32),
             pltpu.VMEM(m_up.shape, f32),
+            pltpu.SemaphoreType.DMA((6,)),
+            pltpu.SemaphoreType.DMA((8 * layers,)),
             pltpu.VMEM(w_down.shape, bf),
             pltpu.VMEM(w_up.shape, bf),
             pltpu.VMEM(m_down.shape, bf),
@@ -550,6 +599,7 @@
             pltpu.SemaphoreType.DMA((row_sems,)),
             pltpu.SemaphoreType.DMA((row_sems,)),
             pltpu.VMEM((tok, width), bf),
+            pltpu.VMEM((width, tok), bf),
             pltpu.VMEM((width, tok), bf),
             pltpu.VMEM((tok, width), f32),
             pltpu.VMEM((layers, tok, rank), f32),
@@ -588,9 +638,10 @@
     means = fused(
         shards, replicas, hidden[0], target[0], w_down[0], w_up[0], m_down[0], m_up[0]
     )
-    if not on_grid(replicas, hidden.shape[2], w_down.shape[3]):
-        totals = lax.psum(tuple(means), "row")
-        means = [total.astype(jnp.float32) / replicas for total in totals]
+    if on_grid(replicas, hidden.shape[2], w_down.shape[3]):
+        return tuple(finish(means))
+    totals = lax.psum(tuple(means), "row")
+    means = [total.astype(jnp.float32) / replicas for total in totals]
     return (
         means[0].astype(jnp.bfloat16),
         means[1].astype(jnp.bfloat16),

time: 155 us -> 149 us (0.961)
  other arithmetic: 3.98 us -> 0 us
  local copies, waits for them, and re-layouts: 2.01 us -> 0 us
    pallas_call x1, Pallas kernels: 148 us -> 143 us  [fused(): pl.pallas_call(functools.partial(fused_kernel, shards, replicas), out_sha...]
    pallas_call x0 -> x1, Pallas kernels: none -> 5.14 us  [finish(): pl.pallas_call(finish_kernel, grid=(layers * parts,), out_shape=[jax.Shap...]
    convert_element_type x2 -> x0, other arithmetic: 3.98 us -> none  [the longest x1 2.63 us: body(): means[2].astype(jnp.float32)]
    unnamed x8 -> x0, local copies, waits for them, and re-layouts: 2.01 us -> none
where the time goes in v3:
time: 149 us; the launch traced here: 148 us
  Pallas kernels  148 us (99%)
    pallas_call x1, Pallas kernels, fused(): pl.pallas_call(functools.partial(fused_kernel, shards, replicas), out_sha...  143 us
    pallas_call x1, Pallas kernels, finish(): pl.pallas_call(finish_kernel, grid=(layers * parts,), out_shape=[jax.Shap...  5.14 us

profile of v3, /device:TPU:0, one launch (start us, length us, event | category | flops | bytes accessed | tf_op | source)
XLA Modules:
  0.0 148.4 jit_solution(11802881185075150489)
XLA Ops:
  0.6 142.6 %shard_map.93 = (bf16[2,896,256]{2,1,0:T(8,128)(2,1)}, bf16[2,256,896]{2,1,0:T(8,128)(2,1)}, bf16[2,896,256]{2,1,0:T(8,128)(2,1)}, bf16[2,256,896]{2,1,0:T(8,128)(2,1)}) custom-call(bf16[256,896]{1,0:T(8,128)(2,1)} %bitcast.10, bf16[256,896]{1,0:T(8,128)(2,1)} %bitcast.11, bf16[2,896,256]{2,1,0:T(8,128)(2,1)} %bitcast.8, bf16[2,256,896]{2,1,0:T(8,128)(2,1)} %bitcast.9, ...), custom_call_target="tpu_custom_call" | custom-call | tf_op jit(solution)/shard_map/pallas_call | solution.py:568
  143.3 5.1 %shard_map.94 = (bf16[2,896,256]{2,1,0:T(8,128)(2,1)}, bf16[2,256,896]{2,1,0:T(8,128)(2,1)}, f32[2,896,256]{2,1,0:T(8,128)}, f32[2,256,896]{2,1,0:T(8,128)}) custom-call(bf16[2,896,256]{2,1,0:T(8,128)(2,1)} %get-tuple-element.8.wd_ref, bf16[2,256,896]{2,1,0:T(8,128)(2,1)} %get-tuple-element.9.wu_ref, bf16[2,896,256]{2,1,0:T(8,128)(2,1)} %get-tuple-element.10.md_ref, ...), custom_call_target="tpu_custom_call" | custom-call | tf_op jit(solution)/shard_map/pallas_call | solution.py:544

commit v4 on v3

--- a/solution.py
+++ b/solution.py
@@ -25,6 +25,19 @@
 LINES = 4
 FOLD_PARTS, LINE_PARTS = 5, 2
 KINDS = 6
+ORDER = [
+    (7, 1), (0, 1), (2, 1), (0, 2), (12, 1), (1, 1), (3, 1), (4, 1), (1, 2), (3, 2), (0, 3), (17, 1), (2, 2),
+    (2, 3), (4, 2), (0, 4), (5, 1), (5, 2), (12, 2), (10, 1), (6, 1), (8, 1), (9, 1), (0, 5), (1, 3), (7, 2),
+    (10, 2), (3, 3), (17, 2), (5, 3), (4, 3), (11, 1), (6, 2), (17, 3), (7, 3), (1, 4), (10, 3), (15, 1),
+    (12, 3), (5, 4), (4, 4), (9, 2), (13, 1), (11, 2), (6, 3), (8, 2), (1, 5), (19, 1), (2, 4), (5, 5),
+    (10, 4), (17, 4), (9, 3), (3, 4), (11, 3), (14, 1), (7, 4), (13, 2), (6, 4), (4, 5), (19, 2), (8, 3),
+    (14, 2), (15, 2), (11, 4), (13, 3), (19, 3), (9, 4), (8, 4), (14, 3), (2, 5), (15, 3), (13, 4), (18, 1),
+    (18, 2), (16, 1), (12, 4), (10, 5), (3, 5), (11, 5), (5, 6), (19, 4), (16, 2), (7, 5), (17, 5), (9, 5),
+    (8, 5), (2, 6), (14, 4), (15, 4), (17, 6), (16, 3), (18, 3), (7, 6), (2, 7), (6, 5), (1, 6), (13, 5),
+    (14, 5), (16, 4), (18, 4), (3, 6), (8, 6), (12, 5), (19, 5), (15, 5), (11, 6), (17, 7), (12, 6), (16, 5),
+    (6, 6), (7, 7), (4, 6), (13, 6), (15, 6), (19, 6), (10, 6), (14, 6), (18, 5), (12, 7), (9, 6), (0, 6),
+    (7, 8), (18, 6), (16, 6), (17, 8), (2, 8), (12, 8),
+]
 
 
 def on_grid(replicas, width, rank):
@@ -35,7 +48,8 @@
     if not wide:
         return [("fold", k * (length // 2), length // 2) for k in range(2)]
     line = length * LINE_PARTS // (FOLD_PARTS + LINE_PARTS) // 128 * 128
-    return [("line", 0, line), ("fold", line, length - line)]
+    size = (length - line) // 2
+    return [("line", 0, line), ("fold", line, size), ("fold", line + size, size)]
 
 
 def fused_kernel(
@@ -44,8 +58,8 @@
     wd_out, wu_out, md_out, mu_out,
     x0_ref, tg_ref, wd, wu, md, mu, load_sem, store_sem, wdl, wul, mdl, mul, res_wd, res_wu, res_md, res_mu,
     got_wd, got_wu, got_md, got_mu, row_send, row_recv,
-    x1, x1t, xt, gr, pre, act, inv, low, proj, slope, gram, sqs,
-    s1, r1, s2, r2, s3, r3, tot, q1, p1, q2, p2, q3, p3,
+    x1, x1t, xt, gr, pre, bend, act, inv, low, proj, slope, gram, sqs,
+    s1, r1, s2, r2, s3, r3, tot, q1, p1, q2, p2,
     main_send, main_recv, side_send, side_recv,
 ):
     tok, width = x0_ref.shape
@@ -59,7 +73,6 @@
     for load in loads:
         load.start()
     full = width * shards
-    half = tok // 2
     chips = shards // 2
     me = lax.axis_index("ta")
     core = lax.rem(me, 2)
@@ -95,11 +108,12 @@
     side = (side_send, side_recv)
     per_channel = 2 + 2 * hops
 
-    def to_row(column):
-        return jnp.broadcast_to(column, (half, half)).T[0:8]
-
     def to_column(row):
-        return jnp.broadcast_to(row[0:1, :], (half, half)).T[:, 0:1]
+        return jnp.broadcast_to(row[0:1, :], (tok, tok)).T[:, 0:1]
+
+    def row_squares(rows):
+        wide = rows.astype(jnp.float32)
+        return dot_nt(jnp.ones((8, width), jnp.bfloat16), (wide * wide).astype(jnp.bfloat16))
 
     class Channel:
         def __init__(self, which):
@@ -118,8 +132,7 @@
             s1[c][...] = tot[c][self.other, :].astype(jnp.bfloat16)
             self.copies = [send(s1[c], r1[c], main, self.base, sibling)]
             if self.squares:
-                sqs[...] = squares
-                q1[...] = to_row(sqs[self.other, :])
+                q1[...] = squares
                 self.copies.append(send(q1, p1, side, 0, sibling))
 
         def cross(self):
@@ -135,8 +148,7 @@
             ]
             tot[c][self.mine, :] = pair
             if self.squares:
-                self.row = to_row(sqs[self.mine, :]) + p1[...]
-                q2[...] = self.row
+                q2[...] = q1[...] + p1[...]
                 self.copies += [
                     send(q2, p2.at[spot], side, 2 + spot, peer)
                     for spot, peer in zip(spots, partners)
@@ -153,20 +165,16 @@
             self.copies = [send(s3[c], r3[c], main, self.base + 1, sibling)]
             tot[c][self.mine, :] = total
             if self.squares:
-                row = self.row
+                row = q2[...]
                 for k in range(hops):
                     row = row + p2[self.parity * hops + k]
-                q3[...] = row
-                self.copies.append(send(q3, p3, side, 1, sibling))
-                sqs[self.mine, :] = to_column(row)
+                sqs[...] = to_column(row)
 
         def end(self):
             c = self.which
             for copy in self.copies:
                 copy.wait()
             tot[c][self.other, :] = r3[c][...].astype(jnp.float32)
-            if self.squares:
-                sqs[self.other, :] = to_column(p3[...])
             return tot[c][...]
 
     forth, own_act, low_act, cross_weight, low_input, first_slope, first_gram = [
@@ -192,12 +200,15 @@
         act[layer] = activation
         return activation
 
-    def low_grads(layer, grad_act):
+    def ready_slope(layer):
         preact = pre[layer]
         sig = jax.nn.sigmoid(preact)
-        grad_pre = grad_act * (sig * (1.0 + preact * (1.0 - sig)))
-        low[layer] = (grad_pre * inv[layer]).astype(jnp.bfloat16)
-        return jnp.sum(grad_pre * preact, axis=1, keepdims=True)
+        steep = sig * (1.0 + preact * (1.0 - sig))
+        bend[layer] = steep * inv[layer]
+        pre[layer] = steep * preact
+
+    def low_grads(layer, grad_act):
+        low[layer] = (grad_act * bend[layer]).astype(jnp.bfloat16)
 
     down, up = (wdl, got_wd, res_wd), (wul, got_wu, res_wu)
     mdown, mup = (mdl, got_md, res_md), (mul, got_mu, res_mu)
@@ -209,7 +220,8 @@
                 for form, base, size in cuts(pair[0].shape[1], wide):
                     chunks.append((pair, layer, form, base, size))
     first = len(chunks) // 2
-    part = first // 4
+    part = len(cuts(width, True))
+    up_part = len(cuts(rank, False))
     sent = []
 
     class Piece:
@@ -377,11 +389,7 @@
 
     pieces = [Piece(k) for k in range(len(chunks))] if levels else []
     done = {k: 0 for k in range(len(chunks))}
-    plan = sorted(
-        (0.25 * (k % first) + (2.0 if k >= first else 0.0) + stage, k, stage)
-        for k, piece in enumerate(pieces)
-        for stage in range(1, piece.stages)
-    )
+    plan = list(ORDER) if levels else []
 
     def start(picked):
         for k in picked if levels else []:
@@ -392,9 +400,9 @@
         for entry in list(plan):
             if taken == count:
                 break
-            if below is not None and entry[1] >= below:
+            if below is not None and entry[0] >= below:
                 continue
-            pieces[entry[1]].run(entry[2])
+            pieces[entry[0]].run(entry[1])
             plan.remove(entry)
             taken += 1
 
@@ -406,20 +414,19 @@
         activation = activate(0, proj[...] * inv[0])
         lifted = dot_nn(activation, wu[0]) * r_scale
         x1[...] = (x0_ref[...].astype(jnp.float32) + lifted).astype(jnp.bfloat16)
-        wide = x1[...].astype(jnp.float32)
-        squares = jnp.sum(wide * wide, axis=1, keepdims=True)
-        forth.begin(parity, dot_nn(x1[...], wd[1]) * d_scale, squares)
+        forth.begin(parity, dot_nn(x1[...], wd[1]) * d_scale, row_squares(x1[...]))
         cross_weight.begin(parity, dot_nn(wu[0], wd[1]) * (r_scale * d_scale))
         forth.cross()
         low_input.begin(parity, dot_nt(x1[...], wu[0]) * r_scale)
         cross_weight.cross()
         low_input.cross()
         x1t[...] = x1[...].T
+        ready_slope(0)
         deferred()
         if last:
             wdl[0] = wd[0]
             start(range(first - part, first))
-            advance(4, first)
+            advance(3, first)
         forth.back()
         forth.end()
         inv[1] = lax.rsqrt(sqs[...] / full + norm_eps)
@@ -432,13 +439,17 @@
         low_act.begin(parity, dot_nt(grad_low, wu[0]) * r_scale)
         own_act.cross()
         low_act.cross()
+        ready_slope(1)
         update_up(1, last)
         cross_weight.back()
         low_input.back()
         if last:
-            advance(6, first)
+            mul[1] = mu[1].astype(jnp.bfloat16)
+            start(range(first, first + up_part))
+            advance(8, first)
         own_act.back()
-        row_dot = low_grads(1, own_act.end())
+        low_grads(1, own_act.end())
+        row_dot = jnp.sum(tot[1][...] * pre[1], axis=1, keepdims=True)
         coefficient = row_dot * inv[1] * inv[1] / full
         through = dot_nt(low[1], wd[1]) * d_scale
         gr[...] = gr[...] + through - coefficient * x1[...].astype(jnp.float32)
@@ -472,8 +483,7 @@
 
     loads[0].wait()
     xt[...] = x0_ref[...].T
-    wide_input = x0_ref[...].astype(jnp.float32)
-    squares = jnp.sum(wide_input * wide_input, axis=1, keepdims=True)
+    squares = row_squares(x0_ref[...])
     loads[1].wait()
     forth.begin(1, dot_nn(x0_ref[...], wd[0]) * d_scale, squares)
     loads[2].wait()
@@ -490,9 +500,9 @@
     lax.fori_loop(0, STEPS - 1, middle, 0)
     step((STEPS - 1) % 2, True, late_down)
     if levels:
-        mul[...] = mu[...].astype(jnp.bfloat16)
         mdl[1] = md[1].astype(jnp.bfloat16)
-        start(range(first, len(chunks) - part))
+        mul[0] = mu[0].astype(jnp.bfloat16)
+        start(range(first + up_part, len(chunks) - part))
     late_down(True)
     mdl[0] = md[0].astype(jnp.bfloat16)
     if not levels:
@@ -553,7 +563,6 @@
 def fused(shards, replicas, hidden, target, w_down, w_up, m_down, m_up):
     tok, width = hidden.shape
     layers, _, rank = w_down.shape
-    half = tok // 2
     hops = shards // 2 - 1
     bf, f32 = jnp.bfloat16, jnp.float32
     hbm = pl.BlockSpec(memory_space=pl.ANY)
@@ -563,7 +572,8 @@
     halves = [pltpu.VMEM((count // 2, rank), bf) for count in rows]
     crossed = [pltpu.VMEM((2 * hops, count // 2, rank), bf) for count in rows]
     totals = [pltpu.VMEM((count, rank), f32) for count in rows]
-    row_sems = 8 * layers * KINDS
+    count = 2 * layers * (len(cuts(rank, False)) + len(cuts(width, True)))
+    row_sems = count * KINDS
     tripled = [(layers, 3 * count, other) for count, other in (w_down.shape[1:], w_up.shape[1:])] * 2
     return pl.pallas_call(
         functools.partial(fused_kernel, shards, replicas),
@@ -583,7 +593,7 @@
             pltpu.VMEM(m_down.shape, f32),
             pltpu.VMEM(m_up.shape, f32),
             pltpu.SemaphoreType.DMA((6,)),
-            pltpu.SemaphoreType.DMA((8 * layers,)),
+            pltpu.SemaphoreType.DMA((count,)),
             pltpu.VMEM(w_down.shape, bf),
             pltpu.VMEM(w_up.shape, bf),
             pltpu.VMEM(m_down.shape, bf),
@@ -603,6 +613,7 @@
             pltpu.VMEM((width, tok), bf),
             pltpu.VMEM((tok, width), f32),
             pltpu.VMEM((layers, tok, rank), f32),
+            pltpu.VMEM((layers, tok, rank), f32),
             pltpu.VMEM((layers, tok, rank), bf),
             pltpu.VMEM((layers, tok, 1), f32),
             pltpu.VMEM((layers, tok, rank), bf),
@@ -617,12 +628,10 @@
             halves,
             halves,
             totals,
-            pltpu.VMEM((8, half), f32),
-            pltpu.VMEM((8, half), f32),
-            pltpu.VMEM((8, half), f32),
-            pltpu.VMEM((2 * hops, 8, half), f32),
-            pltpu.VMEM((8, half), f32),
-            pltpu.VMEM((8, half), f32),
+            pltpu.VMEM((8, tok), f32),
+            pltpu.VMEM((8, tok), f32),
+            pltpu.VMEM((8, tok), f32),
+            pltpu.VMEM((2 * hops, 8, tok), f32),
             pltpu.SemaphoreType.DMA((sems,)),
             pltpu.SemaphoreType.DMA((sems,)),
             pltpu.SemaphoreType.DMA((2 + 2 * hops,)),

time: 149 us -> 141 us (0.946)
  Pallas kernels: 148 us -> 141 us
    pallas_call x1, Pallas kernels: 143 us -> 135 us  [fused(): pl.pallas_call(functools.partial(fused_kernel, shards, replicas), out_sha...]
where the time goes in v4:
time: 141 us
  Pallas kernels  141 us (100%)
    pallas_call x1, Pallas kernels, fused(): pl.pallas_call(functools.partial(fused_kernel, shards, replicas), out_sha...  135 us
    pallas_call x1, Pallas kernels, finish(): pl.pallas_call(finish_kernel, grid=(layers * parts,), out_shape=[jax.Shap...  5.14 us

profile of v4, /device:TPU:0, one launch (start us, length us, event | category | flops | bytes accessed | tf_op | source)
XLA Modules:
  0.0 141.1 jit_solution(2335954237563677512)
XLA Ops:
  0.6 135.4 %shard_map.93 = (bf16[2,896,256]{2,1,0:T(8,128)(2,1)}, bf16[2,256,896]{2,1,0:T(8,128)(2,1)}, bf16[2,896,256]{2,1,0:T(8,128)(2,1)}, bf16[2,256,896]{2,1,0:T(8,128)(2,1)}) custom-call(bf16[256,896]{1,0:T(8,128)(2,1)} %bitcast.10, bf16[256,896]{1,0:T(8,128)(2,1)} %bitcast.11, bf16[2,896,256]{2,1,0:T(8,128)(2,1)} %bitcast.8, bf16[2,256,896]{2,1,0:T(8,128)(2,1)} %bitcast.9, ...), custom_call_target="tpu_custom_call" | custom-call | tf_op jit(solution)/shard_map/pallas_call | solution.py:578
  136.0 5.1 %shard_map.94 = (bf16[2,896,256]{2,1,0:T(8,128)(2,1)}, bf16[2,256,896]{2,1,0:T(8,128)(2,1)}, f32[2,896,256]{2,1,0:T(8,128)}, f32[2,256,896]{2,1,0:T(8,128)}) custom-call(bf16[2,896,256]{2,1,0:T(8,128)(2,1)} %get-tuple-element.8.wd_ref, bf16[2,256,896]{2,1,0:T(8,128)(2,1)} %get-tuple-element.9.wu_ref, bf16[2,896,256]{2,1,0:T(8,128)(2,1)} %get-tuple-element.10.md_ref, ...), custom_call_target="tpu_custom_call" | custom-call | tf_op jit(solution)/shard_map/pallas_call | solution.py:554

commit v5 on v4

--- a/solution.py
+++ b/solution.py
@@ -23,20 +23,20 @@
 
 
 LINES = 4
-FOLD_PARTS, LINE_PARTS = 5, 2
+LINE_SHARE = ((2, 7), (2, 7))
 KINDS = 6
 ORDER = [
-    (7, 1), (0, 1), (2, 1), (0, 2), (12, 1), (1, 1), (3, 1), (4, 1), (1, 2), (3, 2), (0, 3), (17, 1), (2, 2),
-    (2, 3), (4, 2), (0, 4), (5, 1), (5, 2), (12, 2), (10, 1), (6, 1), (8, 1), (9, 1), (0, 5), (1, 3), (7, 2),
-    (10, 2), (3, 3), (17, 2), (5, 3), (4, 3), (11, 1), (6, 2), (17, 3), (7, 3), (1, 4), (10, 3), (15, 1),
-    (12, 3), (5, 4), (4, 4), (9, 2), (13, 1), (11, 2), (6, 3), (8, 2), (1, 5), (19, 1), (2, 4), (5, 5),
-    (10, 4), (17, 4), (9, 3), (3, 4), (11, 3), (14, 1), (7, 4), (13, 2), (6, 4), (4, 5), (19, 2), (8, 3),
-    (14, 2), (15, 2), (11, 4), (13, 3), (19, 3), (9, 4), (8, 4), (14, 3), (2, 5), (15, 3), (13, 4), (18, 1),
-    (18, 2), (16, 1), (12, 4), (10, 5), (3, 5), (11, 5), (5, 6), (19, 4), (16, 2), (7, 5), (17, 5), (9, 5),
-    (8, 5), (2, 6), (14, 4), (15, 4), (17, 6), (16, 3), (18, 3), (7, 6), (2, 7), (6, 5), (1, 6), (13, 5),
-    (14, 5), (16, 4), (18, 4), (3, 6), (8, 6), (12, 5), (19, 5), (15, 5), (11, 6), (17, 7), (12, 6), (16, 5),
-    (6, 6), (7, 7), (4, 6), (13, 6), (15, 6), (19, 6), (10, 6), (14, 6), (18, 5), (12, 7), (9, 6), (0, 6),
-    (7, 8), (18, 6), (16, 6), (17, 8), (2, 8), (12, 8),
+    (0, 1), (0, 2), (2, 1), (1, 1), (5, 1), (3, 1), (4, 1), (7, 1), (0, 3), (6, 1), (1, 2), (3, 2), (2, 2),
+    (2, 3), (5, 2), (4, 2), (1, 3), (3, 3), (7, 2), (8, 1), (12, 1), (1, 4), (6, 2), (0, 4), (17, 1), (5, 3),
+    (10, 1), (4, 3), (9, 1), (8, 2), (6, 3), (11, 1), (13, 1), (12, 2), (3, 4), (15, 1), (10, 2), (14, 1),
+    (18, 1), (16, 1), (4, 4), (0, 5), (1, 5), (7, 3), (17, 2), (2, 4), (12, 3), (9, 2), (11, 2), (8, 3),
+    (4, 5), (5, 4), (17, 3), (5, 5), (6, 4), (13, 2), (9, 3), (19, 1), (11, 3), (10, 3), (8, 4), (14, 2),
+    (0, 6), (13, 3), (9, 4), (12, 4), (15, 2), (3, 5), (7, 4), (10, 4), (18, 2), (16, 2), (2, 5), (4, 6),
+    (17, 4), (9, 5), (13, 4), (15, 3), (6, 5), (10, 5), (19, 2), (2, 6), (11, 4), (15, 4), (18, 3), (11, 5),
+    (14, 3), (7, 5), (2, 7), (5, 6), (16, 3), (1, 6), (12, 5), (18, 4), (19, 3), (7, 6), (9, 6), (3, 6),
+    (14, 4), (12, 6), (17, 5), (8, 5), (15, 5), (16, 4), (17, 6), (2, 8), (18, 5), (11, 6), (19, 4), (6, 6),
+    (12, 7), (14, 5), (7, 7), (17, 7), (10, 6), (13, 5), (16, 5), (19, 5), (15, 6), (7, 8), (18, 6), (13, 6),
+    (8, 6), (12, 8), (16, 6), (19, 6), (14, 6), (17, 8),
 ]
 
 
@@ -44,10 +44,10 @@
     return replicas == 2 * LINES and width % 128 == 0 and rank % 128 == 0 and width >= 512
 
 
-def cuts(length, wide):
+def cuts(length, wide, late):
     if not wide:
         return [("fold", k * (length // 2), length // 2) for k in range(2)]
-    line = length * LINE_PARTS // (FOLD_PARTS + LINE_PARTS) // 128 * 128
+    line = length * LINE_SHARE[late][0] // LINE_SHARE[late][1] // 128 * 128
     size = (length - line) // 2
     return [("line", 0, line), ("fold", line, size), ("fold", line + size, size)]
 
@@ -58,7 +58,7 @@
     wd_out, wu_out, md_out, mu_out,
     x0_ref, tg_ref, wd, wu, md, mu, load_sem, store_sem, wdl, wul, mdl, mul, res_wd, res_wu, res_md, res_mu,
     got_wd, got_wu, got_md, got_mu, row_send, row_recv,
-    x1, x1t, xt, gr, pre, bend, act, inv, low, proj, slope, gram, sqs,
+    x1, x1t, xt, gr, pre, bend, act, inv, low, proj, slope, gram, sqs, ratio,
     s1, r1, s2, r2, s3, r3, tot, q1, p1, q2, p2,
     main_send, main_recv, side_send, side_recv,
 ):
@@ -124,11 +124,12 @@
             self.other = pl.ds(pl.multiple_of((1 - core) * size, size), size)
             self.base = which * per_channel
 
-        def begin(self, parity, value, squares=None):
+        def begin(self, parity, value=None, squares=None):
             c = self.which
             self.parity = parity
             self.squares = squares is not None
-            tot[c][...] = value
+            if value is not None:
+                tot[c][...] = value
             s1[c][...] = tot[c][self.other, :].astype(jnp.bfloat16)
             self.copies = [send(s1[c], r1[c], main, self.base, sibling)]
             if self.squares:
@@ -214,14 +215,14 @@
     mdown, mup = (mdl, got_md, res_md), (mul, got_mu, res_mu)
     layers = list(reversed(range(wd.shape[0])))
     chunks = []
-    for pairs in ((up, down), (mup, mdown)):
+    for late, pairs in enumerate(((up, down), (mup, mdown))):
         for layer in layers:
             for pair, wide in zip(pairs, (False, True)):
-                for form, base, size in cuts(pair[0].shape[1], wide):
+                for form, base, size in cuts(pair[0].shape[1], wide, late):
                     chunks.append((pair, layer, form, base, size))
     first = len(chunks) // 2
-    part = len(cuts(width, True))
-    up_part = len(cuts(rank, False))
+    part = len(cuts(width, True, 0))
+    up_part = len(cuts(rank, False, 0))
     sent = []
 
     class Piece:
@@ -406,11 +407,7 @@
             plan.remove(entry)
             taken += 1
 
-    def step(parity, last, deferred):
-        if last:
-            wul[...] = wu[...]
-            wdl[1] = wd[1]
-            start(range(first - part))
+    def step(parity, last, deferred, nearly=False):
         activation = activate(0, proj[...] * inv[0])
         lifted = dot_nn(activation, wu[0]) * r_scale
         x1[...] = (x0_ref[...].astype(jnp.float32) + lifted).astype(jnp.bfloat16)
@@ -426,38 +423,68 @@
         if last:
             wdl[0] = wd[0]
             start(range(first - part, first))
-            advance(3, first)
+            advance(5, first)
         forth.back()
+        inv[1] = lax.rsqrt(sqs[...] / full + norm_eps)
+
+        def lift(rows):
+            preact = tot[0][rows, :] * inv[1, rows, :]
+            activation = (preact * jax.nn.sigmoid(preact)).astype(jnp.bfloat16)
+            pre[1, rows, :] = preact
+            act[1, rows, :] = activation
+            lifted = dot_nn(activation, wu[1]) * r_scale
+            outcome = (x1[rows, :].astype(jnp.float32) + lifted).astype(jnp.bfloat16)
+            gradient = outcome.astype(jnp.float32) - tg_ref[rows, :].astype(jnp.float32)
+            gr[rows, :] = gradient
+            tot[1][rows, :] = dot_nt(gradient.astype(jnp.bfloat16), wu[1]) * r_scale
+
+        lift(forth.mine)
         forth.end()
-        inv[1] = lax.rsqrt(sqs[...] / full + norm_eps)
-        activation = activate(1, tot[0][...] * inv[1])
-        lifted = dot_nn(activation, wu[1]) * r_scale
-        outcome = (x1[...].astype(jnp.float32) + lifted).astype(jnp.bfloat16)
-        gr[...] = outcome.astype(jnp.float32) - tg_ref[...].astype(jnp.float32)
-        grad_low = gr[...].astype(jnp.bfloat16)
-        own_act.begin(parity, dot_nt(grad_low, wu[1]) * r_scale)
-        low_act.begin(parity, dot_nt(grad_low, wu[0]) * r_scale)
+        lift(forth.other)
+        own_act.begin(parity)
+        low_act.begin(parity, dot_nt(gr[...].astype(jnp.bfloat16), wu[0]) * r_scale)
         own_act.cross()
         low_act.cross()
         ready_slope(1)
         update_up(1, last)
+        if nearly:
+            wul[1] = wu[1]
+            start(range(up_part))
         cross_weight.back()
         low_input.back()
         if last:
             mul[1] = mu[1].astype(jnp.bfloat16)
             start(range(first, first + up_part))
-            advance(8, first)
+            advance(5, first)
         own_act.back()
-        low_grads(1, own_act.end())
-        row_dot = jnp.sum(tot[1][...] * pre[1], axis=1, keepdims=True)
-        coefficient = row_dot * inv[1] * inv[1] / full
-        through = dot_nt(low[1], wd[1]) * d_scale
-        gr[...] = gr[...] + through - coefficient * x1[...].astype(jnp.float32)
+
+        def lower(rows):
+            grad_act = tot[1][rows, :]
+            lowered = (grad_act * bend[1, rows, :]).astype(jnp.bfloat16)
+            low[1, rows, :] = lowered
+            row_dot = jnp.sum(grad_act * pre[1, rows, :], axis=1, keepdims=True)
+            factor = row_dot * inv[1, rows, :] * inv[1, rows, :] / full
+            ratio[rows, :] = factor
+            through = dot_nt(lowered, wd[1]) * d_scale
+            gr[rows, :] = gr[rows, :] + through - factor * x1[rows, :].astype(jnp.float32)
+
+        lower(own_act.mine)
+        own_act.end()
+        lower(own_act.other)
         low_act.back()
         update_up(0, last)
         update_down(1, x1t[...], last)
+        if nearly:
+            wdl[1] = wd[1]
+            wul[0] = wu[0]
+            start(range(up_part, first - part))
+            advance(1, first)
+        if last:
+            mdl[1] = md[1].astype(jnp.bfloat16)
+            mul[0] = mu[0].astype(jnp.bfloat16)
+            start(range(first + up_part, len(chunks) - part))
         weight = cross_weight.end().astype(jnp.bfloat16)
-        grad_act = dot_nt(low[1], weight) - coefficient * low_input.end()
+        grad_act = dot_nt(low[1], weight) - ratio[...] * low_input.end()
         low_grads(0, low_act.end() + grad_act)
         if last:
             return
@@ -497,12 +524,9 @@
     forth.back()
     proj[...] = forth.end()
     inv[0] = lax.rsqrt(sqs[...] / full + norm_eps)
-    lax.fori_loop(0, STEPS - 1, middle, 0)
+    lax.fori_loop(0, STEPS - 2, middle, 0)
+    step(STEPS % 2, False, late_down, nearly=bool(levels))
     step((STEPS - 1) % 2, True, late_down)
-    if levels:
-        mdl[1] = md[1].astype(jnp.bfloat16)
-        mul[0] = mu[0].astype(jnp.bfloat16)
-        start(range(first + up_part, len(chunks) - part))
     late_down(True)
     mdl[0] = md[0].astype(jnp.bfloat16)
     if not levels:
@@ -535,28 +559,53 @@
         store.wait()
 
 
-def finish_kernel(wd_ref, wu_ref, md_ref, mu_ref, wd_out, wu_out, md_out, mu_out):
-    for w_ref, m_ref, w_out, m_out in ((wd_ref, md_ref, wd_out, md_out), (wu_ref, mu_ref, wu_out, mu_out)):
-        moments = m_ref[...].astype(jnp.float32)
-        moved = w_ref[...].astype(jnp.float32) - learn_rate * moments
-        w_out[...] = moved.astype(jnp.bfloat16)
-        m_out[...] = moments
+def finish_kernel(parts, *refs):
+    means, outs, came, made = refs[0:4], refs[4:8], refs[8:12], refs[12:16]
+    load_sem, store_sem = refs[16:]
+    spots = []
+    for layer in range(means[0].shape[0]):
+        for part in range(parts):
+            for pair in range(2):
+                size = means[pair].shape[1] // parts
+                spots.append((pair, layer, pl.ds(part * size, size)))
+
+    def moved(sources, targets, sems, number, which):
+        pair, layer, rows = spots[number]
+        k = pair + which
+        return pltpu.make_async_copy(
+            sources[k].at[layer, rows], targets[k].at[layer, rows], sems.at[2 * number + which // 2]
+        )
+
+    for number in range(len(spots)):
+        for which in (0, 2):
+            moved(means, came, load_sem, number, which).start()
+    for number, (pair, layer, rows) in enumerate(spots):
+        for which in (0, 2):
+            moved(means, came, load_sem, number, which).wait()
+        moments = came[pair + 2][layer, rows, :].astype(jnp.float32)
+        stepped = came[pair][layer, rows, :].astype(jnp.float32) - learn_rate * moments
+        made[pair][layer, rows, :] = stepped.astype(jnp.bfloat16)
+        made[pair + 2][layer, rows, :] = moments
+        for which in (0, 2):
+            moved(made, outs, store_sem, number, which).start()
+    for number in range(len(spots)):
+        for which in (0, 2):
+            moved(made, outs, store_sem, number, which).wait()
 
 
 def finish(means):
-    layers = means[0].shape[0]
     parts = 2
-    specs = [
-        pl.BlockSpec((1, mean.shape[1] // parts, mean.shape[2]), lambda i: (i // parts, i % parts, 0))
-        for mean in means
-    ]
     kinds = [jnp.bfloat16, jnp.bfloat16, jnp.float32, jnp.float32]
+    count = 4 * parts * means[0].shape[0]
+    hbm = pl.BlockSpec(memory_space=pl.ANY)
     return pl.pallas_call(
-        finish_kernel,
-        grid=(layers * parts,),
+        functools.partial(finish_kernel, parts),
         out_shape=[jax.ShapeDtypeStruct(mean.shape, kind) for mean, kind in zip(means, kinds)],
-        in_specs=specs,
-        out_specs=specs,
+        in_specs=[hbm] * 4,
+        out_specs=[hbm] * 4,
+        scratch_shapes=[pltpu.VMEM(mean.shape, mean.dtype) for mean in means]
+        + [pltpu.VMEM(mean.shape, kind) for mean, kind in zip(means, kinds)]
+        + [pltpu.SemaphoreType.DMA((count,)), pltpu.SemaphoreType.DMA((count,))],
     )(*means)
 
 
@@ -572,7 +621,7 @@
     halves = [pltpu.VMEM((count // 2, rank), bf) for count in rows]
     crossed = [pltpu.VMEM((2 * hops, count // 2, rank), bf) for count in rows]
     totals = [pltpu.VMEM((count, rank), f32) for count in rows]
-    count = 2 * layers * (len(cuts(rank, False)) + len(cuts(width, True)))
+    count = 2 * layers * (len(cuts(rank, False, 0)) + len(cuts(width, True, 0)))
     row_sems = count * KINDS
     tripled = [(layers, 3 * count, other) for count, other in (w_down.shape[1:], w_up.shape[1:])] * 2
     return pl.pallas_call(
@@ -621,6 +670,7 @@
             pltpu.VMEM((tok, rank), f32),
             pltpu.VMEM((tok, tok), bf),
             pltpu.VMEM((tok, 1), f32),
+            pltpu.VMEM((tok, 1), f32),
             halves,
             halves,
             halves,

time: 141 us -> 135 us (0.957)
  Pallas kernels: 141 us -> 134 us
    pallas_call x1, Pallas kernels: 135 us -> 130 us  [fused(): pl.pallas_call(functools.partial(fused_kernel, shards, replicas), out_sha...]
where the time goes in v5:
time: 135 us
  Pallas kernels  134 us (99%)
    pallas_call x1, Pallas kernels, fused(): pl.pallas_call(functools.partial(fused_kernel, shards, replicas), out_sha...  130 us
    pallas_call x1, Pallas kernels, finish(): pl.pallas_call(functools.partial(finish_kernel, parts), out_shape=[jax.Sh...  3.81 us

profile of v5, /device:TPU:0, one launch (start us, length us, event | category | flops | bytes accessed | tf_op | source)
XLA Modules:
  0.0 134.7 jit_solution(6379489795465452730)
XLA Ops:
  0.6 130.1 %shard_map.93 = (bf16[2,896,256]{2,1,0:T(8,128)(2,1)}, bf16[2,256,896]{2,1,0:T(8,128)(2,1)}, bf16[2,896,256]{2,1,0:T(8,128)(2,1)}, bf16[2,256,896]{2,1,0:T(8,128)(2,1)}) custom-call(bf16[256,896]{1,0:T(8,128)(2,1)} %bitcast.10, bf16[256,896]{1,0:T(8,128)(2,1)} %bitcast.11, bf16[2,896,256]{2,1,0:T(8,128)(2,1)} %bitcast.8, bf16[2,256,896]{2,1,0:T(8,128)(2,1)} %bitcast.9, ...), custom_call_target="tpu_custom_call" | custom-call | tf_op jit(solution)/shard_map/pallas_call | solution.py:627
  130.7 3.8 %shard_map.94 = (bf16[2,896,256]{2,1,0:T(8,128)(2,1)}, bf16[2,256,896]{2,1,0:T(8,128)(2,1)}, f32[2,896,256]{2,1,0:T(8,128)}, f32[2,256,896]{2,1,0:T(8,128)}) custom-call(bf16[2,896,256]{2,1,0:T(8,128)(2,1)} %get-tuple-element.8.refs_0_, bf16[2,256,896]{2,1,0:T(8,128)(2,1)} %get-tuple-element.9.refs_1_, bf16[2,896,256]{2,1,0:T(8,128)(2,1)} %get-tuple-element.10.refs_2_, ...), custom_call_target="tpu_custom_call" | custom-call | tf_op jit(solution)/shard_map/pallas_call | solution.py:601

commit v6 on v5

--- a/solution.py
+++ b/solution.py
@@ -90,10 +90,15 @@
     line, side_of = spot // 2, lax.rem(spot, 2)
     facing = spot + 1 - 2 * side_of
     after, before = lax.rem(spot + 2, replicas), lax.rem(spot + replicas - 2, replicas)
-    greeted = [facing, after, before] if levels else []
-    for peer in greeted:
+    at_end = (line == 0) | (line == LINES - 1)
+
+    def greet(peer):
         pl.semaphore_signal(barrier, inc=1, device_id={"row": peer}, device_id_type=MESH)
-    pl.semaphore_wait(barrier, chips + len(greeted))
+
+    if levels:
+        greet(facing)
+        pl.when(line < LINES - 1)(lambda: greet(after))
+        pl.when(line > 0)(lambda: greet(before))
 
     def send(src, dst, sems, index, peer):
         copy = pltpu.make_async_remote_copy(
@@ -396,6 +401,17 @@
         for k in picked if levels else []:
             pieces[k].run(0)
 
+    outs = ((wd_out, res_wd, wd), (wu_out, res_wu, wu), (md_out, res_md, mdl), (mu_out, res_mu, mul))
+    stowed = []
+
+    def stow(piece):
+        for out, res, _ in outs:
+            if res is piece.res:
+                stowed.append(pltpu.make_async_copy(
+                    piece.rows(res, 0, piece.size), piece.rows(out, 0, piece.size), store_sem.at[piece.index]
+                ))
+                stowed[-1].start()
+
     def advance(count=None, below=None):
         taken = 0
         for entry in list(plan):
@@ -403,7 +419,10 @@
                 break
             if below is not None and entry[0] >= below:
                 continue
-            pieces[entry[0]].run(entry[1])
+            piece = pieces[entry[0]]
+            piece.run(entry[1])
+            if entry[1] == piece.stages - 1:
+                stow(piece)
             plan.remove(entry)
             taken += 1
 
@@ -510,9 +529,11 @@
 
     loads[0].wait()
     xt[...] = x0_ref[...].T
-    squares = row_squares(x0_ref[...])
+    q1[...] = row_squares(x0_ref[...])
     loads[1].wait()
-    forth.begin(1, dot_nn(x0_ref[...], wd[0]) * d_scale, squares)
+    tot[0][...] = dot_nn(x0_ref[...], wd[0]) * d_scale
+    pl.semaphore_wait(barrier, chips + (jnp.where(at_end, 2, 3) if levels else 0))
+    forth.begin(1, squares=q1[...])
     loads[2].wait()
     first_slope.begin(1, dot_nn(x0_ref[...], md[0].astype(jnp.bfloat16)) * d_scale)
     first_gram.begin(1, dot_nn(x0_ref[...], xt[...]))
@@ -532,7 +553,6 @@
     if not levels:
         mul[...] = mu[...].astype(jnp.bfloat16)
         mdl[1] = md[1].astype(jnp.bfloat16)
-    outs = ((wd_out, res_wd, wd), (wu_out, res_wu, wu), (md_out, res_md, mdl), (mu_out, res_mu, mul))
     if not levels:
         stores = [pltpu.make_async_copy(kept, out, store_sem.at[k]) for k, (out, _, kept) in enumerate(outs)]
         for store in stores:
@@ -542,20 +562,12 @@
         return
     start(range(len(chunks) - part, len(chunks)))
     advance()
-    stores = []
-    for piece in pieces:
-        for out, res, _ in outs:
-            if res is piece.res:
-                stores.append(pltpu.make_async_copy(
-                    piece.rows(res, 0, piece.size), piece.rows(out, 0, piece.size), store_sem.at[piece.index]
-                ))
-                stores[-1].start()
     for when, finish in sent:
         if when is None:
             finish()
         else:
             pl.when(when)(finish)
-    for store in stores:
+    for store in stowed:
         store.wait()
 
 

time: 135 us -> 133 us (0.985)
  Pallas kernels: 134 us -> 132 us
    pallas_call x1, Pallas kernels: 130 us -> 128 us  [fused(): pl.pallas_call(functools.partial(fused_kernel, shards, replicas), out_sha...]
where the time goes in v6:
time: 133 us
  Pallas kernels  132 us (99%)
    pallas_call x1, Pallas kernels, fused(): pl.pallas_call(functools.partial(fused_kernel, shards, replicas), out_sha...  128 us
    pallas_call x1, Pallas kernels, finish(): pl.pallas_call(functools.partial(finish_kernel, parts), out_shape=[jax.Sh...  3.81 us

profile of v6, /device:TPU:0, one launch (start us, length us, event | category | flops | bytes accessed | tf_op | source)
XLA Modules:
  0.0 133.1 jit_solution(230025279700021772)
XLA Ops:
  0.6 128.5 %shard_map.93 = (bf16[2,896,256]{2,1,0:T(8,128)(2,1)}, bf16[2,256,896]{2,1,0:T(8,128)(2,1)}, bf16[2,896,256]{2,1,0:T(8,128)(2,1)}, bf16[2,256,896]{2,1,0:T(8,128)(2,1)}) custom-call(bf16[256,896]{1,0:T(8,128)(2,1)} %bitcast.10, bf16[256,896]{1,0:T(8,128)(2,1)} %bitcast.11, bf16[2,896,256]{2,1,0:T(8,128)(2,1)} %bitcast.8, bf16[2,256,896]{2,1,0:T(8,128)(2,1)} %bitcast.9, ...), custom_call_target="tpu_custom_call" | custom-call | tf_op jit(solution)/shard_map/pallas_call | solution.py:639
  129.1 3.8 %shard_map.94 = (bf16[2,896,256]{2,1,0:T(8,128)(2,1)}, bf16[2,256,896]{2,1,0:T(8,128)(2,1)}, f32[2,896,256]{2,1,0:T(8,128)}, f32[2,256,896]{2,1,0:T(8,128)}) custom-call(bf16[2,896,256]{2,1,0:T(8,128)(2,1)} %get-tuple-element.8.refs_0_, bf16[2,256,896]{2,1,0:T(8,128)(2,1)} %get-tuple-element.9.refs_1_, bf16[2,896,256]{2,1,0:T(8,128)(2,1)} %get-tuple-element.10.refs_2_, ...), custom_call_target="tpu_custom_call" | custom-call | tf_op jit(solution)/shard_map/pallas_call | solution.py:613

commit v7 on v6

--- a/solution.py
+++ b/solution.py
@@ -606,7 +606,7 @@
 
 
 def finish(means):
-    parts = 2
+    parts = 4
     kinds = [jnp.bfloat16, jnp.bfloat16, jnp.float32, jnp.float32]
     count = 4 * parts * means[0].shape[0]
     hbm = pl.BlockSpec(memory_space=pl.ANY)

time: 133 us -> 133 us (level)
  no operation moved by 1% of the time
where the time goes in v7:
time: 133 us
  Pallas kernels  132 us (99%)
    pallas_call x1, Pallas kernels, fused(): pl.pallas_call(functools.partial(fused_kernel, shards, replicas), out_sha...  128 us
    pallas_call x1, Pallas kernels, finish(): pl.pallas_call(functools.partial(finish_kernel, parts), out_shape=[jax.Sh...  3.95 us

profile of v7, /device:TPU:0, one launch (start us, length us, event | category | flops | bytes accessed | tf_op | source)
XLA Modules:
  0.0 133.2 jit_solution(12161689143683020110)
XLA Ops:
  0.6 128.5 %shard_map.93 = (bf16[2,896,256]{2,1,0:T(8,128)(2,1)}, bf16[2,256,896]{2,1,0:T(8,128)(2,1)}, bf16[2,896,256]{2,1,0:T(8,128)(2,1)}, bf16[2,256,896]{2,1,0:T(8,128)(2,1)}) custom-call(bf16[256,896]{1,0:T(8,128)(2,1)} %bitcast.10, bf16[256,896]{1,0:T(8,128)(2,1)} %bitcast.11, bf16[2,896,256]{2,1,0:T(8,128)(2,1)} %bitcast.8, bf16[2,256,896]{2,1,0:T(8,128)(2,1)} %bitcast.9, ...), custom_call_target="tpu_custom_call" | custom-call | tf_op jit(solution)/shard_map/pallas_call | solution.py:639
  129.1 3.9 %shard_map.94 = (bf16[2,896,256]{2,1,0:T(8,128)(2,1)}, bf16[2,256,896]{2,1,0:T(8,128)(2,1)}, f32[2,896,256]{2,1,0:T(8,128)}, f32[2,256,896]{2,1,0:T(8,128)}) custom-call(bf16[2,896,256]{2,1,0:T(8,128)(2,1)} %get-tuple-element.8.refs_0_, bf16[2,256,896]{2,1,0:T(8,128)(2,1)} %get-tuple-element.9.refs_1_, bf16[2,896,256]{2,1,0:T(8,128)(2,1)} %get-tuple-element.10.refs_2_, ...), custom_call_target="tpu_custom_call" | custom-call | tf_op jit(solution)/shard_map/pallas_call | solution.py:613
